TPU v7x, 32 devices: a whole 2x2x4 slice. The times are simulated.
32 devices in a mesh: expert: 8 (over y, x, core), shard: 4 (over z).
Axes of the slice: x: 2, y: 2, z: 4, core: 2. Of those that a mesh axis runs over, the one named last changes fastest.
Arguments:
- states: bfloat16 [18912, 512], P(('expert', 'shard')), may hold values from -6 to 6
- qkv_weight: bfloat16 [2, 512, 1536], P(None, 'shard'), may hold values from -0.25 to 0.25
- out_weight: bfloat16 [2, 512, 512], P(None, 'shard'), may hold values from -0.75 to 0.75
- norm_gain: bfloat16 [2, 512, 2], P(None, 'shard'), may hold values from 0.5 to 1.5
- norm_bias: bfloat16 [2, 512, 2], P(None, 'shard'), may hold values from -1.5 to 1.5
- router_weight: bfloat16 [2, 512, 32], P(None, 'shard'), may hold values from -0.25 to 0.25
- expert_in: bfloat16 [2, 32, 512, 2048], P(None, 'expert', 'shard'), may hold values from -0.25 to 0.25
- expert_out: bfloat16 [2, 32, 2048, 512], P(None, 'expert', 'shard'), may hold values from -2 to 2
- chosen: int32 [2, 18912, 2], P(None, ('expert', 'shard')), may hold values from 0 to 31, all different within a row; in each aligned block of 591 rows (0 to 590, 591 to 1181, ..., all dimensions but the last counted through in order) at most 74 rows name the same one
- image_count: int32 [32], P(('expert', 'shard')), may hold values from 2 to 3
- teacher: bfloat16 [18912, 512], P(('expert', 'shard')), may hold values from -6 to 6
Outputs:
- final_states: bfloat16 [18912, 512], P(('expert', 'shard'))
- input_grad: float32 [18912, 512], P(('expert', 'shard'))
- qkv_grad: float32 [2, 512, 1536], P(None, 'shard')
- out_grad: float32 [2, 512, 512], P(None, 'shard')
- gain_grad: float32 [2, 512, 2], P(None, 'shard')
- bias_grad: float32 [2, 512, 2], P(None, 'shard')
- router_grad: float32 [2, 512, 32], P(None, 'shard')
- expert_in_grad: float32 [2, 32, 512, 2048], P(None, 'expert', 'shard')
- expert_out_grad: float32 [2, 32, 2048, 512], P(None, 'expert', 'shard')
Inputs may be any that keep to these rules, and one draw needn't show every extreme that they name: `chosen`: in each block the 591 rows of one device name every expert at most 74 times, and in each block some device names some expert exactly 74 times; the two experts of a token differ. Device i, counted in the order of the expert axis then the shard axis, holds image_count[i] live images in its first image slots; its other slots are padding: their rows of final_states are computed like any other row, but the loss and every gradient ignore them.
All inputs are finite; a program needn't handle non-finite values.
Results may differ from a plain program's by a relative error of at most 0.012.
Values may be sent and summed in bfloat16 or wider, within the bound.
A program may use at most 256 MiB of HBM per device.

v0:
```python
import jax
import jax.numpy as jnp
from jax import lax
from jax.sharding import PartitionSpec as P

HEADS = 8
HEAD_DIM = 64
EXPERTS = 32
TOP = 2
SEQ = 197
SLOTS = 3
CAP = 74


norm_eps = 1e-06


def layer_norm(values, gain_row, shift_row):
    centred = values - jnp.mean(values, axis=-1, keepdims=True)
    spread = jnp.mean(centred * centred, axis=-1, keepdims=True)
    return centred * lax.rsqrt(spread + norm_eps) * gain_row + shift_row


def route_slots(picks_dev, capacity):
    flat_ids = picks_dev.reshape(-1)
    onehot = (flat_ids[:, None] == jnp.arange(EXPERTS, dtype=jnp.int32)[None, :]).astype(jnp.int32)
    before = jnp.cumsum(onehot, axis=0) - onehot
    ranking = jnp.sum(before * onehot, axis=1)
    slot_index = flat_ids * capacity + ranking
    routes_dev = flat_ids.shape[0]
    source = jnp.full((EXPERTS * capacity,), routes_dev, jnp.int32)
    source = source.at[slot_index].set(jnp.arange(routes_dev, dtype=jnp.int32))
    return (slot_index, source)


def attention_forward(current, qkv_full, out_full, gain_row, shift_row):
    model_width = current.shape[1]
    normed = layer_norm(current, gain_row, shift_row).astype(jnp.bfloat16)
    projected = jnp.dot(normed, qkv_full, preferred_element_type=jnp.float32).astype(jnp.bfloat16)
    split_parts = projected.reshape(SLOTS, SEQ, 3, HEADS, HEAD_DIM)
    scores = jnp.einsum(
        "ashd,athd->ahst",
        split_parts[:, :, 0],
        split_parts[:, :, 1],
        preferred_element_type=jnp.float32,
    ) * HEAD_DIM ** (-0.5)
    highest_score = jnp.max(scores, axis=-1, keepdims=True)
    exponent = jnp.exp(scores - highest_score)
    summed = jnp.sum(exponent, axis=-1, keepdims=True)
    weights = (exponent / summed).astype(jnp.bfloat16)
    log_total = highest_score + jnp.log(summed)
    attended = jnp.einsum(
        "ahst,athd->ashd", weights, split_parts[:, :, 2], preferred_element_type=jnp.float32
    )
    attended = attended.reshape(SLOTS * SEQ, model_width).astype(jnp.bfloat16)
    branch_out = jnp.dot(attended, out_full, preferred_element_type=jnp.float32)
    return (current + branch_out, (current, normed, projected, log_total, attended))


def attention_backward(grad_states, saved, qkv_full, out_full, gain_row, shift_row):
    current, normed, projected, log_total, attended = saved
    model_width = current.shape[1]
    grad_branch = grad_states.astype(jnp.bfloat16)
    grad_out = jnp.einsum("rd,re->de", attended, grad_branch, preferred_element_type=jnp.float32)
    grad_attended = jnp.einsum(
        "re,de->rd", grad_branch, out_full, preferred_element_type=jnp.float32
    ).astype(jnp.bfloat16)
    split_parts = projected.reshape(SLOTS, SEQ, 3, HEADS, HEAD_DIM)
    queries = split_parts[:, :, 0]
    keys_part = split_parts[:, :, 1]
    values_part = split_parts[:, :, 2]
    scaling = HEAD_DIM ** (-0.5)
    scores = (
        jnp.einsum("ashd,athd->ahst", queries, keys_part, preferred_element_type=jnp.float32)
        * scaling
    )
    chances = jnp.exp(scores - log_total)
    grad_heads = grad_attended.reshape(SLOTS, SEQ, HEADS, HEAD_DIM)
    grad_weights = jnp.einsum(
        "ashd,athd->ahst", grad_heads, values_part, preferred_element_type=jnp.float32
    )
    grad_values = jnp.einsum(
        "ahst,ashd->athd",
        chances.astype(jnp.bfloat16),
        grad_heads,
        preferred_element_type=jnp.float32,
    )
    centre_term = jnp.sum(grad_weights * chances, axis=-1, keepdims=True)
    grad_scores = (chances * (grad_weights - centre_term)).astype(jnp.bfloat16)
    grad_queries = (
        jnp.einsum("ahst,athd->ashd", grad_scores, keys_part, preferred_element_type=jnp.float32)
        * scaling
    )
    grad_keys = (
        jnp.einsum("ahst,ashd->athd", grad_scores, queries, preferred_element_type=jnp.float32)
        * scaling
    )
    grad_projected = jnp.stack([grad_queries, grad_keys, grad_values], axis=2)
    grad_projected = grad_projected.reshape(SLOTS * SEQ, 3 * model_width).astype(jnp.bfloat16)
    grad_qkv = jnp.einsum("rd,re->de", normed, grad_projected, preferred_element_type=jnp.float32)
    grad_normed = jnp.einsum(
        "re,de->rd", grad_projected, qkv_full, preferred_element_type=jnp.float32
    )
    unused_value, norm_pullback = jax.vjp(layer_norm, current, gain_row, shift_row)
    grad_input, grad_gain, grad_shift = norm_pullback(grad_normed)
    return (grad_states + grad_input, grad_qkv, grad_out, grad_gain, grad_shift)


def mixture_forward(current, gain_row, shift_row, router_full, in_shard, out_shard, picks_layer):
    row_count, model_width = current.shape
    experts_all = router_full.shape[1]
    normed = layer_norm(current, gain_row, shift_row).astype(jnp.bfloat16)
    logits = jnp.dot(normed, router_full, preferred_element_type=jnp.float32)
    chances = jax.nn.softmax(logits, axis=-1)
    matches = picks_layer[:, :, None] == jnp.arange(experts_all, dtype=jnp.int32)[None, None, :]
    gate_values = jnp.sum(jnp.where(matches, chances[:, None, :], 0.0), axis=-1)
    slot_index, source = route_slots(picks_layer, CAP)
    filled = source < TOP * row_count
    route_clip = jnp.minimum(source, TOP * row_count - 1)
    taken_rows = route_clip // TOP
    outgoing = jnp.where(filled[:, None], normed[taken_rows], jnp.zeros((), jnp.bfloat16))
    outgoing = outgoing.reshape(experts_all, CAP, model_width)
    arrived = lax.all_to_all(outgoing, "expert", split_axis=0, concat_axis=1, tiled=True)
    in_full, out_full = (
        lax.all_gather(in_shard, "shard", axis=1, tiled=True),
        lax.all_gather(out_shard, "shard", axis=1, tiled=True),
    )
    hidden_pre = jnp.einsum("erd,edh->erh", arrived, in_full, preferred_element_type=jnp.float32)
    activated = jax.nn.gelu(hidden_pre).astype(jnp.bfloat16)
    produced = jnp.einsum(
        "erh,ehd->erd", activated, out_full, preferred_element_type=jnp.float32
    ).astype(jnp.bfloat16)
    returned = lax.all_to_all(produced, "expert", split_axis=1, concat_axis=0, tiled=True)
    routed = returned.reshape(experts_all * CAP, model_width)[slot_index].reshape(
        row_count, TOP, model_width
    )
    updated = current + jnp.sum(gate_values[:, :, None] * routed.astype(jnp.float32), axis=1)
    saved = (
        current,
        normed,
        chances,
        matches,
        gate_values,
        slot_index,
        filled,
        route_clip,
        arrived,
        routed,
        in_full,
        out_full,
    )
    return (updated, saved)


def mixture_backward(grad_states, saved, gain_row, shift_row, router_full, in_shard, out_shard):
    (
        current,
        normed,
        chances,
        matches,
        gate_values,
        slot_index,
        filled,
        route_clip,
        arrived,
        routed,
        kept_in,
        kept_out,
    ) = saved
    row_count, model_width = current.shape
    experts_all = chances.shape[1]
    grad_routed = (gate_values[:, :, None] * grad_states[:, None, :]).astype(jnp.bfloat16)
    grad_routed = grad_routed.reshape(TOP * row_count, model_width)
    grad_gates = jnp.sum(grad_states[:, None, :] * routed.astype(jnp.float32), axis=-1)
    grad_outgoing = jnp.where(filled[:, None], grad_routed[route_clip], jnp.zeros((), jnp.bfloat16))
    grad_outgoing = grad_outgoing.reshape(experts_all, CAP, model_width)
    grad_result = lax.all_to_all(grad_outgoing, "expert", split_axis=0, concat_axis=1, tiled=True)
    in_full, out_full = (
        lax.all_gather(in_shard, "shard", axis=1, tiled=True),
        lax.all_gather(out_shard, "shard", axis=1, tiled=True),
    )
    hidden_pre = jnp.einsum("erd,edh->erh", arrived, in_full, preferred_element_type=jnp.float32)
    activated, gelu_pullback = jax.vjp(jax.nn.gelu, hidden_pre)
    grad_out_experts = jnp.einsum(
        "erh,erd->ehd",
        activated.astype(jnp.bfloat16),
        grad_result,
        preferred_element_type=jnp.float32,
    )
    grad_activated = jnp.einsum(
        "erd,ehd->erh", grad_result, out_full, preferred_element_type=jnp.float32
    )
    grad_pre = gelu_pullback(grad_activated)[0].astype(jnp.bfloat16)
    grad_in_experts = jnp.einsum(
        "erd,erh->edh", arrived, grad_pre, preferred_element_type=jnp.float32
    )
    grad_arrived = jnp.einsum(
        "erh,edh->erd", grad_pre, in_full, preferred_element_type=jnp.float32
    ).astype(jnp.bfloat16)
    grad_returned = lax.all_to_all(grad_arrived, "expert", split_axis=1, concat_axis=0, tiled=True)
    grad_in_share, grad_out_share = (
        lax.psum_scatter(
            grad_in_experts.astype(jnp.bfloat16), "shard", scatter_dimension=1, tiled=True
        ).astype(jnp.float32),
        lax.psum_scatter(
            grad_out_experts.astype(jnp.bfloat16), "shard", scatter_dimension=1, tiled=True
        ).astype(jnp.float32),
    )
    grad_routes = grad_returned.reshape(experts_all * CAP, model_width)[slot_index]
    grad_normed = jnp.sum(
        grad_routes.reshape(row_count, TOP, model_width).astype(jnp.float32), axis=1
    )
    grad_chances = jnp.sum(jnp.where(matches, grad_gates[:, :, None], 0.0), axis=1)
    grad_logits = chances * (grad_chances - jnp.sum(grad_chances * chances, axis=-1, keepdims=True))
    grad_logits = grad_logits.astype(jnp.bfloat16)
    grad_router = jnp.einsum("rd,re->de", normed, grad_logits, preferred_element_type=jnp.float32)
    grad_normed = grad_normed + jnp.einsum(
        "re,de->rd", grad_logits, router_full, preferred_element_type=jnp.float32
    )
    unused_value, norm_pullback = jax.vjp(layer_norm, current, gain_row, shift_row)
    grad_input, grad_gain, grad_shift = norm_pullback(grad_normed)
    return (
        grad_states + grad_input,
        grad_router,
        grad_gain,
        grad_shift,
        grad_in_share,
        grad_out_share,
    )


def shards(
    states,
    qkv_weight,
    out_weight,
    norm_gain,
    norm_bias,
    router_weight,
    expert_in,
    expert_out,
    chosen,
    image_count,
    teacher,
):
    qkv_full, out_full, gain_full, bias_full, router_full = (
        lax.all_gather(qkv_weight, "shard", axis=1, tiled=True),
        lax.all_gather(out_weight, "shard", axis=1, tiled=True),
        lax.all_gather(norm_gain, "shard", axis=1, tiled=True),
        lax.all_gather(norm_bias, "shard", axis=1, tiled=True),
        lax.all_gather(router_weight, "shard", axis=1, tiled=True),
    )
    gain_float = gain_full.astype(jnp.float32)
    bias_float = bias_full.astype(jnp.float32)
    layer_count = qkv_weight.shape[0]
    row_count, model_width = states.shape
    slot_image = jnp.arange(row_count, dtype=jnp.int32) // SEQ
    living = slot_image < image_count[0]
    counted = lax.psum(image_count[0].astype(jnp.float32) * SEQ, ("expert", "shard"))
    current = states.astype(jnp.float32)
    attention_kept = []
    mixture_kept = []
    for layer_index in range(layer_count):
        current, kept_attention = attention_forward(
            current,
            qkv_full[layer_index],
            out_full[layer_index],
            gain_float[layer_index, :, 0],
            bias_float[layer_index, :, 0],
        )
        current, kept_mixture = mixture_forward(
            current,
            gain_float[layer_index, :, 1],
            bias_float[layer_index, :, 1],
            router_full[layer_index],
            expert_in[layer_index],
            expert_out[layer_index],
            chosen[layer_index],
        )
        attention_kept.append(kept_attention)
        mixture_kept.append(kept_mixture)
    missed = current - teacher.astype(jnp.float32)
    grad_states = jnp.where(living[:, None], 2.0 * missed, 0.0) / counted
    qkv_list = [None] * layer_count
    out_list = [None] * layer_count
    gain_list = [None] * layer_count
    bias_list = [None] * layer_count
    router_list = [None] * layer_count
    in_list = [None] * layer_count
    experts_out_list = [None] * layer_count
    for layer_index in reversed(range(layer_count)):
        grad_states, grad_router, gain_second, shift_second, grad_in_share, grad_out_share = (
            mixture_backward(
                grad_states,
                mixture_kept[layer_index],
                gain_float[layer_index, :, 1],
                bias_float[layer_index, :, 1],
                router_full[layer_index],
                expert_in[layer_index],
                expert_out[layer_index],
            )
        )
        grad_states, grad_qkv, grad_out, gain_first, shift_first = attention_backward(
            grad_states,
            attention_kept[layer_index],
            qkv_full[layer_index],
            out_full[layer_index],
            gain_float[layer_index, :, 0],
            bias_float[layer_index, :, 0],
        )
        qkv_list[layer_index] = grad_qkv
        out_list[layer_index] = grad_out
        gain_list[layer_index] = jnp.stack([gain_first, gain_second], axis=-1)
        bias_list[layer_index] = jnp.stack([shift_first, shift_second], axis=-1)
        router_list[layer_index] = grad_router
        in_list[layer_index] = grad_in_share
        experts_out_list[layer_index] = grad_out_share
    mixer_grads = (
        jnp.stack(qkv_list),
        jnp.stack(out_list),
        jnp.stack(gain_list),
        jnp.stack(bias_list),
        jnp.stack(router_list),
    )
    summed = lax.psum(
        (mixer_grads[0], mixer_grads[1], mixer_grads[2], mixer_grads[3], mixer_grads[4]),
        ("expert", "shard"),
    )
    share_width = model_width // lax.axis_size("shard")
    start_index = lax.axis_index("shard") * share_width
    reduced = tuple(
        (lax.dynamic_slice_in_dim(member, start_index, share_width, 1) for member in summed)
    )
    return (
        current.astype(jnp.bfloat16),
        grad_states * counted,
        reduced[0],
        reduced[1],
        reduced[2],
        reduced[3],
        reduced[4],
        jnp.stack(in_list),
        jnp.stack(experts_out_list),
    )


def solution(mesh):
    in_specs = (
        P(("expert", "shard"), None),
        P(None, "shard", None),
        P(None, "shard", None),
        P(None, "shard", None),
        P(None, "shard", None),
        P(None, "shard", None),
        P(None, "expert", "shard", None),
        P(None, "expert", "shard", None),
        P(None, ("expert", "shard"), None),
        P(("expert", "shard")),
        P(("expert", "shard"), None),
    )
    out_specs = (
        P(("expert", "shard"), None),
        P(("expert", "shard"), None),
        P(None, "shard", None),
        P(None, "shard", None),
        P(None, "shard", None),
        P(None, "shard", None),
        P(None, "shard", None),
        P(None, "expert", "shard", None),
        P(None, "expert", "shard", None),
    )
    return jax.shard_map(shards, mesh=mesh, in_specs=in_specs, out_specs=out_specs, check_vma=False)
```

profile of v0, /device:TPU:0, one launch (start us, length us, event | category | flops | bytes accessed | tf_op | source)
XLA Modules:
  0.0 1961.3 jit_solution(13753770390396414759)
XLA Ops:
  8.7 4.8 fusion.155
  13.6 4.5 fusion.156
  20.2 9.1 reduce-window.14
  30.1 6.4 scatter_custom_fusion
  36.7 13.1 all_gather.31
  49.8 8.6 all_gather.32
  60.7 15.1 all-gather.11.cloned.1.call-done
  78.5 3.8 reshape.514
  96.6 7.5 all-gather.13.cloned.1.call-done
  107.0 8.1 gather_fusion
  124.5 31.3 %all-to-all-done = bf16[32,74,512]{2,1,0:T(8,128)(2,1)S(1)} async-done(((bf16[32,74,512]{2,1,0:T(8,128)(2,1)}), bf16[32,74,512]{2,1,0:T(8,128)(2,1)S(1)}, u32[]{:S(2)}, u32[]{:S(2)}) %all-to-all-start) | async-done | bytes 2424864 | tf_op jit(solution)/shard_map/all_to_all | solution.py:123
  159.1 95.6 %all-gather.15.cloned.1.call-done = bf16[1,4,512,2048]{3,2,1,0:T(8,128)(2,1)} async-done(((bf16[1,4,128,2048]{3,2,1,0:T(8,128)(2,1)}), bf16[1,4,512,2048]{3,2,1,0:T(8,128)(2,1)}) %all-gather.15.cloned.1.call-update) | async-done | bytes 8388624 | tf_op jit(solution)/shard_map/all_gather | solution.py:125
  254.7 14.4 fusion.28
  269.1 134.8 %all-gather.17.cloned.1.call-done = bf16[1,4,2048,512]{3,2,1,0:T(8,128)(2,1)} async-done(((bf16[1,4,512,512]{3,2,1,0:T(8,128)(2,1)}), bf16[1,4,2048,512]{3,2,1,0:T(8,128)(2,1)}) %all-gather.17.cloned.1.call-update) | async-done | bytes 8388624 | tf_op jit(solution)/shard_map/all_gather | solution.py:126
  403.9 13.5 fusion.63
  425.5 9.1 reduce-window.16
  438.0 6.4 scatter_custom_fusion.1
  445.1 21.0 %all_gather.35 = bf16[2,512,32]{1,2,0:T(8,128)(2,1)S(1)} all-gather(bf16[2,128,32]{1,2,0:T(8,128)(2,1)} %param.16), channel_id=1, replica_groups=mesh['expert'=8,'shard'=4] {'shard'}, dimensions={1}, use_global_device_ids=true | all-gather | bytes 81920 | tf_op jit(solution)/shard_map/all_gather | solution.py:250
  473.8 4.7 gather_fusion.1
  481.4 12.4 multiply_reduce_fusion.7
  519.0 8.1 gather_fusion.2
  531.0 35.6 %all_to_all.132 = bf16[32,74,512]{2,1,0:T(8,128)(2,1)S(1)} all-to-all(bf16[32,74,512]{2,1,0:T(8,128)(2,1)S(1)} %broadcast_select_fusion.1), channel_id=1, replica_groups=mesh['expert'=8,'shard'=4] {'expert'}, dimensions={0} | all-to-all | bytes 4849664 | tf_op jit(solution)/shard_map/all_to_all | solution.py:123
  568.5 13.6 fusion.20
  582.1 121.3 %all-gather.21.cloned.1.call-done = bf16[1,4,2048,512]{3,2,1,0:T(8,128)(2,1)} async-done(((bf16[1,4,512,512]{3,2,1,0:T(8,128)(2,1)}), bf16[1,4,2048,512]{3,2,1,0:T(8,128)(2,1)}) %all-gather.21.cloned.1.call-update) | async-done | bytes 8388624 | tf_op jit(solution)/shard_map/all_gather | solution.py:126
  703.4 12.8 fusion.69
  724.1 60.8 %psum.42 = f32[]{:T(128)} all-reduce(f32[]{:T(128)S(6)} %mul.550), channel_id=1, replica_groups=mesh['expert'=8,'shard'=4] {'expert','shard'}, use_global_device_ids=true, to_apply=%region_28.29 | all-reduce | flops 1 | bytes 8 | tf_op jit(solution)/shard_map/psum | solution.py:258
  791.2 4.7 gather_fusion.3
  798.9 12.4 multiply_reduce_fusion.6
  820.0 8.2 gather_fusion.4
  831.4 36.2 %all_to_all.133 = bf16[32,74,512]{2,1,0:T(8,128)(2,1)S(1)} all-to-all(bf16[32,74,512]{2,1,0:T(8,128)(2,1)S(1)} %broadcast_select_fusion), channel_id=1, replica_groups=mesh['expert'=8,'shard'=4] {'expert'}, dimensions={0} | all-to-all | bytes 4849664 | tf_op jit(solution)/shard_map/all_to_all | solution.py:177
  869.5 22.3 %fusion.13 = bf16[4,592,2048]{2,1,0:T(8,128)(2,1)} fusion(f32[4,592,2048]{2,1,0:T(8,128)} %fusion.20, bf16[1,4,2048,512]{3,2,1,0:T(8,128)(2,1)} %all-gather.21.cloned.1.call-done, bf16[4,592,512]{2,0,1:T(4,128)(2,1)S(1)} %bitcast.291), kind=kOutput, calls=%fused_computation.27 | convolution fusion | flops 5063049216 | bytes 39911424 | tf_op jit(solution)/shard_map/erd,ehd->erh/dot_general | solution.py:190
  891.9 10.3 fusion.66
  905.6 4.7 all-to-all-start.5
  913.4 27.0 %all-to-all-done.5 = bf16[4,592,512]{2,0,1:T(4,128)(2,1)} async-done(((bf16[4,592,512]{2,0,1:T(4,128)(2,1)}), bf16[4,592,512]{2,0,1:T(4,128)(2,1)}, u32[]{:S(2)}, u32[]{:S(2)}) %all-to-all-start.5) | async-done | bytes 2424864 | tf_op jit(solution)/shard_map/all_to_all | solution.py:200
  940.4 3.9 copy.269
  947.1 4.7 gather_fusion.5
  955.6 4.6 reduce_sum.427
  971.4 3.9 multiply_reduce_fusion.1
  978.7 3.9 copy.277
  982.6 7.0 convert_element_type.253
  989.7 4.2 multiply_reduce_fusion.9
  1001.5 8.1 gather_fusion.6
  1012.9 35.1 %all_to_all.134 = bf16[32,74,512]{2,1,0:T(8,128)(2,1)S(1)} all-to-all(bf16[32,74,512]{2,1,0:T(8,128)(2,1)S(1)} %broadcast_select_fusion.2), channel_id=1, replica_groups=mesh['expert'=8,'shard'=4] {'expert'}, dimensions={0} | all-to-all | bytes 4849664 | tf_op jit(solution)/shard_map/all_to_all | solution.py:177
  1049.9 22.3 %fusion.6 = bf16[4,592,2048]{2,1,0:T(8,128)(2,1)} fusion(f32[4,592,2048]{2,1,0:T(8,128)} %fusion.28, bf16[1,4,2048,512]{3,2,1,0:T(8,128)(2,1)} %all-gather.17.cloned.1.call-done, bf16[4,592,512]{2,0,1:T(4,128)(2,1)S(1)} %bitcast.293), kind=kOutput, calls=%fused_computation.20 | convolution fusion | flops 5063049216 | bytes 39911424 | tf_op jit(solution)/shard_map/erd,ehd->erh/dot_general | solution.py:190
  1072.2 10.3 fusion.60
  1085.8 4.6 all-to-all-start.7
  1101.3 19.3 all-to-all-done.7
  1127.2 4.7 gather_fusion.7
  1135.8 4.6 reduce_sum.442
  1150.7 3.9 multiply_reduce_fusion
  1158.0 3.9 copy.291
  1161.9 7.0 convert_element_type.265
  1178.2 16.9 convolution_convert_fusion
  1195.2 15.5 convolution_convert_fusion.1
  1210.8 13.5 convolution_convert_fusion.2
  1224.3 13.1 convolution_convert_fusion.3
  1242.4 37.4 %all-reduce.2 = (f32[2,512,2]{1,2,0:T(2,128)S(1)}, f32[2,512,2]{1,2,0:T(2,128)S(1)}) all-reduce(f32[2,512,2]{1,2,0:T(2,128)S(1)} %pad_maximum_fusion.3, f32[2,512,2]{1,2,0:T(2,128)S(1)} %pad_maximum_fusion.4), channel_id=1, replica_groups=mesh['expert'=8,'shard'=4] {'expert','shard'}, use_global_device_ids=true, to_apply=%region_53.54 | all-reduce | flops 4096 | bytes 32768 | tf_op jit(solution)/shard_map/psum | solution.py:324
  1283.2 74.4 %all-reduce.6.cloned.1.call-done = (f32[2,512,1536]{2,1,0:T(8,128)}, f32[2,512,512]{2,1,0:T(8,128)}, f32[2,512,32]{1,2,0:T(8,128)}) async-done(((f32[2,512,1536]{2,1,0:T(8,128)}, f32[2,512,512]{2,1,0:T(8,128)}, f32[2,512,32]{1,2,0:T(8,128)}), (f32[2,512,1536]{2,1,0:T(8,128)}, f32[2,512,512]{2,1,0:T(8,128)}, f32[2,512,32]{1,2,0:T(8,128)})) %all-reduce.6.cloned.1.call-update) | async-done | bytes 8519696 | tf_op jit(solution)/shard_map/psum | solution.py:324
  1363.4 141.7 %reduce-scatter.11.cloned.1.call-done = bf16[4,512,512]{2,1,0:T(8,128)(2,1)} async-done(((bf16[4,2048,512]{2,1,0:T(8,128)(2,1)}), bf16[4,512,512]{2,1,0:T(8,128)(2,1)}) %reduce-scatter.11.cloned.1.call-update) | async-done | bytes 2097168 | tf_op jit(solution)/shard_map/reduce_scatter | solution.py:205
  1505.1 147.7 %reduce-scatter.9.cloned.1.call-done = bf16[4,512,512]{2,1,0:T(8,128)(2,1)} async-done(((bf16[4,2048,512]{2,1,0:T(8,128)(2,1)}), bf16[4,512,512]{2,1,0:T(8,128)(2,1)}) %reduce-scatter.9.cloned.1.call-update) | async-done | bytes 2097168 | tf_op jit(solution)/shard_map/reduce_scatter | solution.py:205
  1652.8 6.2 maximum_convert_fusion.3
  1659.0 141.9 %reduce-scatter.7.cloned.1.call-done = bf16[4,128,2048]{2,1,0:T(8,128)(2,1)} async-done(((bf16[4,512,2048]{2,1,0:T(8,128)(2,1)}), bf16[4,128,2048]{2,1,0:T(8,128)(2,1)}) %reduce-scatter.7.cloned.1.call-update) | async-done | bytes 2097168 | tf_op jit(solution)/shard_map/reduce_scatter | solution.py:202
  1800.8 147.6 %reduce-scatter.5.cloned.1.call-done = bf16[4,128,2048]{2,1,0:T(8,128)(2,1)} async-done(((bf16[4,512,2048]{2,1,0:T(8,128)(2,1)}), bf16[4,128,2048]{2,1,0:T(8,128)(2,1)}) %reduce-scatter.5.cloned.1.call-update) | async-done | bytes 2097168 | tf_op jit(solution)/shard_map/reduce_scatter | solution.py:202
  1948.5 6.2 maximum_convert_fusion.2
  (496 shorter events, 223.9 us)
Async XLA Ops:
  7.2 68.7 %all-gather.11.cloned.1.call-start = ((), (), s32[]{:S(2)}) async-start(), calls=%async_computation.12 | async-start | bytes 3932160 | tf_op jit(solution)/shard_map/all_gather | solution.py:246
  7.9 96.2 %all-gather.13.cloned.1.call-start = ((), (), s32[]{:S(2)}) async-start(), calls=%async_computation.13 | async-start | bytes 1310720 | tf_op jit(solution)/shard_map/all_gather | solution.py:247
  8.7 246.0 %all-gather.15.cloned.1.call-start = ((), (), s32[]{:S(2)}) async-start(), calls=%async_computation.18 | async-start | bytes 10485760 | tf_op jit(solution)/shard_map/all_gather | solution.py:125
  13.5 390.4 %all-gather.17.cloned.1.call-start = ((), (), s32[]{:S(2)}) async-start(), calls=%async_computation.19 | async-start | bytes 10485760 | tf_op jit(solution)/shard_map/all_gather | solution.py:126
  18.1 550.4 %all-gather.19.cloned.1.call-start = ((), (), s32[]{:S(2)}) async-start(), calls=%async_computation.20 | async-start | bytes 10485760 | tf_op jit(solution)/shard_map/all_gather | solution.py:125
  18.8 17.9 copy-start.127
  18.8 31.0 %copy-start.128 = (bf16[2,128,2]{1,2,0:T(2,128)(2,1)S(1)}, bf16[2,128,2]{1,2,0:T(2,128)(2,1)}, u32[]{:S(2)}) copy-start(bf16[2,128,2]{1,2,0:T(2,128)(2,1)} %param.15) | copy-start | bytes 3076
  18.8 40.2 %copy-start.25 = (bf16[591,512]{1,0:T(8,128)(2,1)S(1)}, bf16[591,512]{1,0:T(8,128)(2,1)}, u32[]{:S(2)}) copy-start(bf16[591,512]{1,0:T(8,128)(2,1)} %param.11) | copy-start | bytes 1815556
  30.1 19.7 %copy-start.108 = (s32[1182]{0:T(1024)}, s32[1182]{0:T(1024)S(1)}, u32[]{:S(2)}) copy-start(s32[1182]{0:T(1024)S(1)} %fusion.133) | copy-start | bytes 14188
  36.7 81.4 %copy-start.101 = (pred[32,74]{1,0:T(8,128)(4,1)}, pred[32,74]{1,0:T(8,128)(4,1)S(1)}, u32[]{:S(2)}) copy-start(pred[32,74]{1,0:T(8,128)(4,1)S(1)} %broadcast_in_dim.169) | copy-start | bytes 7108
  59.2 19.3 copy-start.82
  59.5 19.0 copy-start.91
  59.5 19.0 copy-start.99
  60.1 18.4 copy-start.123
  60.7 17.8 copy-start.111
  60.7 46.0 %copy-start.104 = (f32[1,512,1]{1,2,0:T(1,128)}, f32[1,512,1]{1,2,0:T(1,128)S(1)}, u32[]{:S(2)}) copy-start(f32[1,512,1]{1,2,0:T(1,128)S(1)} %get-tuple-element.59) | copy-start | bytes 6148
  96.6 10.4 copy-start.36
  107.0 360.4 %copy-start = (bf16[591,512]{1,0:T(8,128)(2,1)}, bf16[591,512]{1,0:T(8,128)(2,1)S(1)}, u32[]{:S(2)}) copy-start(bf16[591,512]{1,0:T(8,128)(2,1)S(1)} %add_convert_fusion.2) | copy-start | bytes 1815556
  119.8 35.9 %all-to-all-start = ((bf16[32,74,512]{2,1,0:T(8,128)(2,1)}), bf16[32,74,512]{2,1,0:T(8,128)(2,1)S(1)}, u32[]{:S(2)}, u32[]{:S(2)}) async-start(bf16[32,74,512]{2,1,0:T(8,128)(2,1)} %broadcast_select_fusion.3), calls=%async_computation | async-start | bytes 5242880 | tf_op jit(solution)/shard_map/all_to_all | solution.py:123
  123.5 579.9 %all-gather.21.cloned.1.call-start = ((), (), s32[]{:S(2)}) async-start(), calls=%async_computation.21 | async-start | bytes 10485760 | tf_op jit(solution)/shard_map/all_gather | solution.py:126
  124.4 299.9 %copy-start.75 = (s32[1182]{0:T(1024)}, s32[1182]{0:T(1024)S(1)}, u32[]{:S(2)}) copy-start(s32[1182]{0:T(1024)S(1)} %eq.89) | copy-start | bytes 14188
  420.7 47.9 %all-to-all-start.1 = ((bf16[4,592,512]{2,0,1:T(4,128)(2,1)}), bf16[4,592,512]{2,0,1:T(4,128)(2,1)S(1)}, u32[]{:S(2)}, u32[]{:S(2)}) async-start(bf16[4,592,512]{2,0,1:T(4,128)(2,1)} %copy.246), calls=%async_computation.1 | async-start | bytes 4849664 | tf_op jit(solution)/shard_map/all_to_all | solution.py:133
  435.5 33.0 %copy-start.86 = (s32[591,2]{0,1:T(2,128)S(1)}, s32[591,2]{0,1:T(2,128)}, u32[]{:S(2)}) copy-start(s32[591,2]{0,1:T(2,128)} %get-tuple-element.52) | copy-start | bytes 14188
  437.9 7.2 copy-start.109
  466.9 6.9 copy-start.71
  481.4 12.7 copy-start.12
  481.4 12.4 copy-start.7
  519.0 265.9 %copy-start.2 = (bf16[591,512]{1,0:T(8,128)(2,1)}, bf16[591,512]{1,0:T(8,128)(2,1)S(1)}, u32[]{:S(2)}) copy-start(bf16[591,512]{1,0:T(8,128)(2,1)S(1)} %add_convert_fusion) | copy-start | bytes 1815556
  568.5 13.7 copy-start.27
  719.6 65.3 %copy-start.110 = (s32[1182]{0:T(1024)S(1)}, s32[1182]{0:T(1024)}, u32[]{:S(2)}) copy-start(s32[1182]{0:T(1024)} %copy-done.109) | copy-start | bytes 14188
  719.6 65.3 %copy-start.57 = (bf16[2,512,32]{1,2,0:T(8,128)(2,1)S(1)}, bf16[2,512,32]{1,2,0:T(8,128)(2,1)}, u32[]{:S(2)}) copy-start(bf16[2,512,32]{1,2,0:T(8,128)(2,1)} %copy-done.56) | copy-start | bytes 196612
  719.6 65.7 %copy-start.88 = (s32[591,2]{0,1:T(2,128)S(1)}, s32[591,2]{0,1:T(2,128)}, u32[]{:S(2)}) copy-start(s32[591,2]{0,1:T(2,128)} %get-tuple-element.51) | copy-start | bytes 14188
  719.6 66.1 %all-to-all-start.3 = ((bf16[4,592,512]{2,0,1:T(4,128)(2,1)}), bf16[4,592,512]{2,0,1:T(4,128)(2,1)S(1)}, u32[]{:S(2)}, u32[]{:S(2)}) async-start(bf16[4,592,512]{2,0,1:T(4,128)(2,1)} %copy.262), calls=%async_computation.3 | async-start | bytes 4849664 | tf_op jit(solution)/shard_map/all_to_all | solution.py:133
  784.9 6.3 copy-start.73
  798.8 14.3 copy-start.14
  798.8 12.4 copy-start.10
  798.9 12.4 copy-start.55
  869.5 22.3 %copy-start.50 = (bf16[8,4,74,512]{3,1,2,0:T(4,128)(2,1)}, bf16[8,4,74,512]{3,1,2,0:T(4,128)(2,1)S(1)}, u32[]{:S(2)}) copy-start(bf16[8,4,74,512]{3,1,2,0:T(4,128)(2,1)S(1)} %copy.309) | copy-start | bytes 7274500
  905.5 4.9 copy-start.70
  905.6 4.9 copy-start.15
  905.6 34.8 %all-to-all-start.5 = ((bf16[4,592,512]{2,0,1:T(4,128)(2,1)}), bf16[4,592,512]{2,0,1:T(4,128)(2,1)}, u32[]{:S(2)}, u32[]{:S(2)}) async-start(bf16[4,592,512]{2,0,1:T(4,128)(2,1)} %copy.268), calls=%async_computation.5 | async-start | bytes 4849664 | tf_op jit(solution)/shard_map/all_to_all | solution.py:200
  963.4 31.0 %copy-start.24 = (f32[591,512]{1,0:T(8,128)}, f32[591,512]{1,0:T(8,128)S(1)}, u32[]{:S(2)}) copy-start(f32[591,512]{1,0:T(8,128)S(1)} %add_add_fusion.6) | copy-start | bytes 3631108
  967.8 7.5 slice-start.2
  982.6 7.0 copy-start.18
  982.6 7.0 copy-start.90
  982.6 7.0 copy-start.114
  982.6 7.1 copy-start.119
  1049.9 22.3 %copy-start.51 = (bf16[8,4,74,512]{3,1,2,0:T(4,128)(2,1)}, bf16[8,4,74,512]{3,1,2,0:T(4,128)(2,1)S(1)}, u32[]{:S(2)}) copy-start(bf16[8,4,74,512]{3,1,2,0:T(4,128)(2,1)S(1)} %copy.311) | copy-start | bytes 7274500
  1085.8 4.9 copy-start.60
  1085.8 4.9 copy-start.68
  1085.8 4.9 copy-start.3
  1085.8 5.2 copy-start.13
  1085.8 34.8 %all-to-all-start.7 = ((bf16[4,592,512]{2,0,1:T(4,128)(2,1)}), bf16[4,592,512]{2,0,1:T(4,128)(2,1)}, u32[]{:S(2)}, u32[]{:S(2)}) async-start(bf16[4,592,512]{2,0,1:T(4,128)(2,1)} %copy.282), calls=%async_computation.7 | async-start | bytes 4849664 | tf_op jit(solution)/shard_map/all_to_all | solution.py:200
  1090.5 267.1 %all-reduce.6.cloned.1.call-start = ((), (), s32[]{:S(2)}) async-start(), calls=%async_computation.22 | async-start | bytes 17039360 | tf_op jit(solution)/shard_map/psum | solution.py:324
  1147.1 7.5 slice-start
  1161.9 7.0 copy-start.26
  1161.9 7.0 copy-start.83
  1161.9 7.0 copy-start.100
  1161.9 7.0 copy-start.112
  1161.9 7.0 copy-start.124
  1178.2 327.0 %reduce-scatter.11.cloned.1.call-start = ((), (), s32[]{:S(2)}) async-start(), calls=%async_computation.17 | async-start | bytes 10485760 | tf_op jit(solution)/shard_map/reduce_scatter | solution.py:205
  1195.1 457.7 %reduce-scatter.9.cloned.1.call-start = ((), (), s32[]{:S(2)}) async-start(), calls=%async_computation.16 | async-start | bytes 10485760 | tf_op jit(solution)/shard_map/reduce_scatter | solution.py:205
  1210.7 590.1 %reduce-scatter.7.cloned.1.call-start = ((), (), s32[]{:S(2)}) async-start(), calls=%async_computation.15 | async-start | bytes 10485760 | tf_op jit(solution)/shard_map/reduce_scatter | solution.py:202
  1224.3 724.2 %reduce-scatter.5.cloned.1.call-start = ((), (), s32[]{:S(2)}) async-start(), calls=%async_computation.14 | async-start | bytes 10485760 | tf_op jit(solution)/shard_map/reduce_scatter | solution.py:202
  (86 other events, 199.2 us)
Sparse Core Ops, SparseCore 0:
  9.6 66.2 all-gather.10
  77.4 26.5 all-gather.12
  105.6 148.9 all-gather.14
  256.1 147.7 all-gather.16
  405.3 148.7 all-gather.18
  555.6 147.7 all-gather.20
  1178.3 179.2 all-reduce.5
  1360.5 144.6 reduce-scatter.10
  1507.5 145.2 reduce-scatter.8
  1655.6 145.2 reduce-scatter.6
  1803.2 145.2 reduce-scatter.4
where the time goes:
time: 1970 us; the launch traced here: 1960 us
  waiting for transfers between devices  1110 us (56%)
  blocking collectives  248 us (13%)
  local copies, waits for them, and re-layouts  234 us (12%)
  matrix products  231 us (12%)
  other arithmetic  103 us (5%)
  starting transfers between devices  21.2 us (1%)
    reduce_scatter x2, waiting for transfers between devices, mixture_backward(): lax.psum_scatter(grad_in_experts.astype(jnp.bfloat16), 'shard', scatter_d...  290 us
    reduce_scatter x2, waiting for transfers between devices, mixture_backward(): lax.psum_scatter(grad_out_experts.astype(jnp.bfloat16), 'shard', scatter_...  289 us
    all_gather x2, waiting for transfers between devices, mixture_forward(): lax.all_gather(out_shard, 'shard', axis=1, tiled=True)  256 us
    all_gather x2, waiting for transfers between devices, mixture_forward(): lax.all_gather(in_shard, 'shard', axis=1, tiled=True)  95.6 us
    psum x1, waiting for transfers between devices, shards(): lax.psum((mixer_grads[0], mixer_grads[1], mixer_grads[2], mixer_grads[3],...  74.4 us
    all_to_all x2, blocking collectives, mixture_backward(): lax.all_to_all(grad_outgoing, 'expert', split_axis=0, concat_axis=1, tile...  71.3 us
    psum x1, blocking collectives, shards(): lax.psum(image_count[0].astype(jnp.float32) * SEQ, ('expert', 'shard'))  60.8 us
    all_to_all x2, waiting for transfers between devices, mixture_backward(): lax.all_to_all(grad_arrived, 'expert', split_axis=1, concat_axis=0, tiled...  46.3 us
  transfers between devices with their start and end apart: 16, of which 13 were waited for; matrix products, arithmetic and copies ran while one was open for 15% of the time, Pallas kernels for 0%

commit v1 on v0

--- a/solution.py
+++ b/solution.py
@@ -1,6 +1,8 @@
 import jax
 import jax.numpy as jnp
 from jax import lax
+from jax.experimental import pallas as pl
+from jax.experimental.pallas import tpu as pltpu
 from jax.sharding import PartitionSpec as P
 
 HEADS = 8
@@ -10,9 +12,531 @@
 SEQ = 197
 SLOTS = 3
 CAP = 74
-
-
 norm_eps = 1e-06
+
+LANES = 128
+SEQ_PAD = 208
+ROWS = 640
+CAP_PAD = 80
+CHUNK = 64
+F32 = jnp.float32
+BF16 = jnp.bfloat16
+
+
+def dot(a, b):
+    return jnp.dot(a, b, preferred_element_type=F32)
+
+
+def dot_nt(a, b):
+    return lax.dot_general(a, b, (((1,), (1,)), ((), ())), preferred_element_type=F32)
+
+
+def dot_tn(a, b):
+    return lax.dot_general(a, b, (((0,), (0,)), ((), ())), preferred_element_type=F32)
+
+
+def rows_of(step, size):
+    return pl.ds(pl.multiple_of(step * size, size), size)
+
+
+def each_chunk(body, size=CHUNK, total=ROWS):
+    def step(i, carry):
+        body(rows_of(i, size))
+        return carry
+
+    lax.fori_loop(0, total // size, step, 0)
+
+
+def centre(values):
+    centred = values - jnp.mean(values, axis=-1, keepdims=True)
+    spread = jnp.mean(centred * centred, axis=-1, keepdims=True)
+    return centred, lax.rsqrt(spread + norm_eps)
+
+
+def norm_rows(x_ref, gain, shift, out_ref):
+    def body(rows):
+        centred, inverse = centre(x_ref[rows, :])
+        out_ref[rows, :] = (centred * inverse * gain + shift).astype(BF16)
+
+    each_chunk(body)
+
+
+def norm_pullback(x_ref, gain, grad_ref, total_ref, out_ref, sums_ref):
+    sums_ref[...] = jnp.zeros_like(sums_ref)
+
+    def body(rows):
+        centred, inverse = centre(x_ref[rows, :])
+        unit = centred * inverse
+        grad = grad_ref[rows, :]
+        scaled = grad * gain
+        first = jnp.mean(scaled, axis=-1, keepdims=True)
+        second = jnp.mean(scaled * unit, axis=-1, keepdims=True)
+        out_ref[rows, :] = total_ref[rows, :] + inverse * (scaled - first - unit * second)
+        sums_ref[0:1, :] += jnp.sum(grad * unit, axis=0, keepdims=True)
+        sums_ref[1:2, :] += jnp.sum(grad, axis=0, keepdims=True)
+
+    each_chunk(body)
+
+
+def weight_parts(w_ref, model):
+    side = jnp.transpose(w_ref[:, 4 * model :].astype(F32))
+    return [side[EXPERTS + i : EXPERTS + i + 1, :] for i in range(4)]
+
+
+def attention_rows(x_ref, w_ref, gain, shift, x1_ref, proj_ref, log_ref, att_ref, normed_ref):
+    model = x_ref.shape[1]
+    norm_rows(x_ref, gain, shift, normed_ref)
+    for part in range(3):
+        columns = slice(part * model, (part + 1) * model)
+        proj_ref[:, columns] = dot(normed_ref[...], w_ref[:, columns]).astype(BF16)
+    att_ref[...] = jnp.zeros_like(att_ref)
+    log_ref[...] = jnp.zeros_like(log_ref)
+    low = lax.broadcasted_iota(jnp.int32, (SEQ_PAD, LANES), 1) < HEAD_DIM
+    inside = lax.broadcasted_iota(jnp.int32, (SEQ_PAD, SEQ_PAD), 1) < SEQ
+    lane = lax.broadcasted_iota(jnp.int32, (SEQ_PAD, LANES), 1)
+
+    def image(i, carry):
+        rows = rows_of(i, SEQ_PAD)
+        logs = jnp.zeros((SEQ_PAD, LANES), F32)
+        for pair in range(HEADS // 2):
+            at = pair * LANES
+            queries = proj_ref[rows, at : at + LANES]
+            keys = proj_ref[rows, model + at : model + at + LANES]
+            values = proj_ref[rows, 2 * model + at : 2 * model + at + LANES]
+            results = []
+            for side in range(2):
+                mine = low if side == 0 else jnp.logical_not(low)
+                masked = jnp.where(mine, queries, jnp.zeros_like(queries))
+                scores = dot_nt(masked, keys) * HEAD_DIM ** (-0.5)
+                scores = jnp.where(inside, scores, -1e30)
+                highest = jnp.max(scores, axis=-1, keepdims=True)
+                exponent = jnp.exp(scores - highest)
+                summed = jnp.sum(exponent, axis=-1, keepdims=True)
+                weights = (exponent / summed).astype(BF16)
+                logs = jnp.where(lane == 2 * pair + side, highest + jnp.log(summed), logs)
+                results.append(dot(weights, values))
+            att_ref[rows, at : at + LANES] = jnp.where(low, results[0], results[1]).astype(BF16)
+        log_ref[rows, :] = logs
+        return carry
+
+    lax.fori_loop(0, SLOTS, image, 0)
+    x1_ref[...] = x_ref[...] + dot(att_ref[...], w_ref[:, 3 * model : 4 * model])
+
+
+def route_rows(picks_ref, slots_ref, turned_ref):
+    lane = lax.broadcasted_iota(jnp.int32, (ROWS, LANES), 1)
+    picks = picks_ref[...]
+    firsts, seconds = picks[:, 0:1], picks[:, 1:2]
+    match_first, match_second = lane == firsts, lane == seconds
+    either = jnp.where(match_first | match_second, 1.0, 0.0).astype(BF16)
+    down = lax.broadcasted_iota(jnp.int32, (ROWS, ROWS), 0)
+    across = lax.broadcasted_iota(jnp.int32, (ROWS, ROWS), 1)
+    before = dot(jnp.where(across < down, 1.0, 0.0).astype(BF16), either)
+    rank_first = jnp.sum(jnp.where(match_first, before, 0.0), axis=-1, keepdims=True)
+    rank_second = jnp.sum(jnp.where(match_second, before, 0.0), axis=-1, keepdims=True)
+    slot_first = jnp.where(firsts < 0, -1.0, firsts.astype(F32) * CAP_PAD + rank_first)
+    slot_second = jnp.where(seconds < 0, -1.0, seconds.astype(F32) * CAP_PAD + rank_second)
+    both = jnp.where(lane == 0, slot_first, jnp.where(lane == 1, slot_second, -1.0))
+    slots_ref[...] = both.astype(jnp.int32)
+    turned_ref[...] = jnp.transpose(both)[0:8, :].astype(jnp.int32)
+
+
+def gate_rows(normed_ref, w_ref, picks_ref, chances_ref, gates_ref):
+    model = normed_ref.shape[1]
+    lane = lax.broadcasted_iota(jnp.int32, (ROWS, LANES), 1)
+    logits = dot(normed_ref[...], w_ref[:, 4 * model :])
+    logits = jnp.where(lane < EXPERTS, logits, -1e30)
+    exponent = jnp.exp(logits - jnp.max(logits, axis=-1, keepdims=True))
+    chances = exponent / jnp.sum(exponent, axis=-1, keepdims=True)
+    chances_ref[...] = chances
+    picks = picks_ref[...]
+    gate_first = jnp.sum(jnp.where(lane == picks[:, 0:1], chances, 0.0), axis=-1, keepdims=True)
+    gate_second = jnp.sum(jnp.where(lane == picks[:, 1:2], chances, 0.0), axis=-1, keepdims=True)
+    gates_ref[...] = jnp.where(lane == 0, gate_first, jnp.where(lane == 1, gate_second, 0.0))
+
+
+BLOCK = 4 * CAP_PAD
+
+
+def dispatch_rows(turned_ref, rows_ref, out_ref):
+    def block(i, carry):
+        slot = lax.broadcasted_iota(jnp.int32, (BLOCK, ROWS), 0) + i * BLOCK
+        chosen = (slot == turned_ref[0:1, :]) | (slot == turned_ref[1:2, :])
+        out_ref[rows_of(i, BLOCK), :] = dot(
+            jnp.where(chosen, 1.0, 0.0).astype(BF16), rows_ref[...]
+        ).astype(BF16)
+        return carry
+
+    lax.fori_loop(0, EXPERTS * CAP_PAD // BLOCK, block, 0)
+
+
+def dispatch_pairs(turned_ref, pairs_ref, out_ref):
+    def block(i, carry):
+        slot = lax.broadcasted_iota(jnp.int32, (BLOCK, ROWS), 0) + i * BLOCK
+        first = jnp.where(slot == turned_ref[0:1, :], 1.0, 0.0).astype(BF16)
+        second = jnp.where(slot == turned_ref[1:2, :], 1.0, 0.0).astype(BF16)
+        out_ref[rows_of(i, BLOCK), :] = dot(
+            jnp.concatenate([first, second], axis=1), pairs_ref[...]
+        ).astype(BF16)
+        return carry
+
+    lax.fori_loop(0, EXPERTS * CAP_PAD // BLOCK, block, 0)
+
+
+PART = 512
+
+
+def collect_pairs(slots_ref, returned_ref, total_ref):
+    total_ref[...] = jnp.zeros_like(total_ref)
+
+    def part(i, carry):
+        slot = lax.broadcasted_iota(jnp.int32, (ROWS, PART), 1) + i * PART
+        rows = returned_ref[rows_of(i, PART), :]
+        for side in range(2):
+            chosen = jnp.where(slot == slots_ref[:, side : side + 1], 1.0, 0.0).astype(BF16)
+            total_ref[side * ROWS : (side + 1) * ROWS, :] += dot(chosen, rows)
+        return carry
+
+    lax.fori_loop(0, EXPERTS * CAP_PAD // PART, part, 0)
+
+
+def collect_sums(slots_ref, returned_ref, total_ref):
+    total_ref[...] = jnp.zeros_like(total_ref)
+
+    def part(i, carry):
+        slot = lax.broadcasted_iota(jnp.int32, (ROWS, PART), 1) + i * PART
+        chosen = (slot == slots_ref[:, 0:1]) | (slot == slots_ref[:, 1:2])
+        total_ref[...] += dot(
+            jnp.where(chosen, 1.0, 0.0).astype(BF16), returned_ref[rows_of(i, PART), :]
+        )
+        return carry
+
+    lax.fori_loop(0, EXPERTS * CAP_PAD // PART, part, 0)
+
+
+def combine(x1_ref, gates_ref, slots_ref, returned_ref, x_ref, routed_ref, total_ref):
+    collect_pairs(slots_ref, returned_ref, total_ref)
+
+    def body(rows):
+        later = pl.ds(pl.multiple_of(rows.start + ROWS, CHUNK), CHUNK)
+        first, second = total_ref[rows, :], total_ref[later, :]
+        gates = gates_ref[rows, :]
+        x_ref[rows, :] = x1_ref[rows, :] + gates[:, 0:1] * first + gates[:, 1:2] * second
+        routed_ref[rows, :] = first.astype(BF16)
+        routed_ref[later, :] = second.astype(BF16)
+
+    each_chunk(body)
+
+
+def split_grads(grad_ref, gates_ref, routed_ref, turned_ref, pairs_ref, grad_gates_ref, out_ref):
+    lane = lax.broadcasted_iota(jnp.int32, (CHUNK, LANES), 1)
+
+    def body(rows):
+        later = pl.ds(pl.multiple_of(rows.start + ROWS, CHUNK), CHUNK)
+        grad = grad_ref[rows, :]
+        gates = gates_ref[rows, :]
+        pairs_ref[rows, :] = (gates[:, 0:1] * grad).astype(BF16)
+        pairs_ref[later, :] = (gates[:, 1:2] * grad).astype(BF16)
+        first = jnp.sum(grad * routed_ref[rows, :].astype(F32), axis=-1, keepdims=True)
+        second = jnp.sum(grad * routed_ref[later, :].astype(F32), axis=-1, keepdims=True)
+        grad_gates_ref[rows, :] = jnp.where(lane == 0, first, jnp.where(lane == 1, second, 0.0))
+
+    each_chunk(body)
+    dispatch_pairs(turned_ref, pairs_ref, out_ref)
+
+
+def attention_pullback(grad_ref, w_ref, proj_ref, log_ref, att_ref, normed_ref, small_ref, gproj_ref, gatt_ref, back_ref, gnormed_ref):
+    model = grad_ref.shape[1]
+
+    def body(rows):
+        back_ref[rows, :] = grad_ref[rows, :].astype(BF16)
+
+    each_chunk(body)
+    small_ref[:, 3 * model : 4 * model] = dot_tn(att_ref[...], back_ref[...])
+    gatt_ref[...] = dot_nt(back_ref[...], w_ref[:, 3 * model : 4 * model]).astype(BF16)
+    gproj_ref[SLOTS * SEQ_PAD :, :] = jnp.zeros((ROWS - SLOTS * SEQ_PAD, 3 * model), BF16)
+    low = lax.broadcasted_iota(jnp.int32, (SEQ_PAD, LANES), 1) < HEAD_DIM
+    inside = lax.broadcasted_iota(jnp.int32, (SEQ_PAD, SEQ_PAD), 1) < SEQ
+    scaling = HEAD_DIM ** (-0.5)
+
+    def image(i, carry):
+        rows = rows_of(i, SEQ_PAD)
+        for pair in range(HEADS // 2):
+            at = pair * LANES
+            queries = proj_ref[rows, at : at + LANES]
+            keys = proj_ref[rows, model + at : model + at + LANES]
+            values = proj_ref[rows, 2 * model + at : 2 * model + at + LANES]
+            grad_heads = gatt_ref[rows, at : at + LANES]
+            parts = []
+            for side in range(2):
+                mine = low if side == 0 else jnp.logical_not(low)
+                zero = jnp.zeros_like(queries)
+                head = 2 * pair + side
+                scores = dot_nt(jnp.where(mine, queries, zero), keys) * scaling
+                chances = jnp.where(inside, jnp.exp(scores - log_ref[rows, head : head + 1]), 0.0)
+                grad_weights = dot_nt(jnp.where(mine, grad_heads, zero), values)
+                centre_term = jnp.sum(grad_weights * chances, axis=-1, keepdims=True)
+                grad_scores = (chances * (grad_weights - centre_term)).astype(BF16)
+                parts.append(
+                    (
+                        dot(grad_scores, keys) * scaling,
+                        dot_tn(grad_scores, queries) * scaling,
+                        dot_tn(chances.astype(BF16), grad_heads),
+                    )
+                )
+            for which in range(3):
+                to = which * model + at
+                gproj_ref[rows, to : to + LANES] = jnp.where(low, parts[0][which], parts[1][which]).astype(BF16)
+        return carry
+
+    lax.fori_loop(0, SLOTS, image, 0)
+    for part in range(3):
+        columns = slice(part * model, (part + 1) * model)
+        small_ref[:, columns] = dot_tn(normed_ref[...], gproj_ref[:, columns])
+    gnormed_ref[...] = dot_nt(gproj_ref[...], w_ref[:, : 3 * model])
+
+
+def router_pullback(grad_gates_ref, picks_ref, chances_ref, w_ref, normed_ref, gnormed_ref, router_ref):
+    model = normed_ref.shape[1]
+    lane = lax.broadcasted_iota(jnp.int32, (ROWS, LANES), 1)
+    picks, grads, chances = picks_ref[...], grad_gates_ref[...], chances_ref[...]
+    spread = jnp.where(lane == picks[:, 0:1], grads[:, 0:1], 0.0) + jnp.where(lane == picks[:, 1:2], grads[:, 1:2], 0.0)
+    logits = chances * (spread - jnp.sum(spread * chances, axis=-1, keepdims=True))
+    logits = logits.astype(BF16)
+    router_ref[...] = dot_tn(normed_ref[...], logits)
+    gnormed_ref[...] += dot_nt(logits, w_ref[:, 4 * model :])
+
+
+def front(x_ref, w_ref, picks_ref, outs, scratch):
+    x1_ref, proj_ref, log_ref, att_ref, slots_ref, turned_ref, chances_ref, gates_ref, leaving_ref = outs
+    (normed_ref,) = scratch
+    gain1, gain2, shift1, shift2 = weight_parts(w_ref, x_ref.shape[1])
+    attention_rows(x_ref, w_ref, gain1, shift1, x1_ref, proj_ref, log_ref, att_ref, normed_ref)
+    route_rows(picks_ref, slots_ref, turned_ref)
+    norm_rows(x1_ref, gain2, shift2, normed_ref)
+    gate_rows(normed_ref, w_ref, picks_ref, chances_ref, gates_ref)
+    dispatch_rows(turned_ref, normed_ref, leaving_ref)
+
+
+def first_kernel(x_ref, w_ref, picks_ref, *rest):
+    front(x_ref, w_ref, picks_ref, rest[:9], rest[9:])
+
+
+def middle_kernel(x1_ref, gates_ref, slots_ref, returned_ref, w_ref, picks_ref, x_ref, routed_ref, *rest):
+    combine(x1_ref, gates_ref, slots_ref, returned_ref, x_ref, routed_ref, rest[10])
+    front(x_ref, w_ref, picks_ref, rest[:9], rest[9:10])
+
+
+def last_kernel(x1_ref, gates_ref, slots_ref, turned_ref, returned_ref, teacher_ref, scale_ref, final_ref, grad_ref, grad_gates_ref, leaving_ref, x_ref, routed_ref, total_ref, pairs_ref):
+    combine(x1_ref, gates_ref, slots_ref, returned_ref, x_ref, routed_ref, total_ref)
+
+    def body(rows):
+        values = x_ref[rows, :]
+        final_ref[rows, :] = values.astype(BF16)
+        grad_ref[rows, :] = (values - teacher_ref[rows, :].astype(F32)) * scale_ref[rows, :]
+
+    each_chunk(body)
+    split_grads(grad_ref, gates_ref, routed_ref, turned_ref, pairs_ref, grad_gates_ref, leaving_ref)
+
+
+def back(grad_in_ref, returned_ref, slots_ref, picks_ref, grad_gates_ref, chances_ref, x1_ref, x_ref, proj_ref, log_ref, att_ref, w_ref, grad_ref, small_ref, scratch):
+    normed_ref, gnormed_ref, gproj_ref, gatt_ref, back_ref, mid_ref, sums_a, sums_b, router_ref = scratch
+    model = x_ref.shape[1]
+    gain1, gain2, shift1, shift2 = weight_parts(w_ref, model)
+    collect_sums(slots_ref, returned_ref, gnormed_ref)
+    norm_rows(x1_ref, gain2, shift2, normed_ref)
+    router_pullback(grad_gates_ref, picks_ref, chances_ref, w_ref, normed_ref, gnormed_ref, router_ref)
+    norm_pullback(x1_ref, gain2, gnormed_ref, grad_in_ref, mid_ref, sums_b)
+    norm_rows(x_ref, gain1, shift1, normed_ref)
+    attention_pullback(mid_ref, w_ref, proj_ref, log_ref, att_ref, normed_ref, small_ref, gproj_ref, gatt_ref, back_ref, gnormed_ref)
+    norm_pullback(x_ref, gain1, gnormed_ref, mid_ref, grad_ref, sums_a)
+    rows = lax.broadcasted_iota(jnp.int32, (LANES, model), 0)
+    side = jnp.zeros((LANES, model), F32)
+    for i, value in enumerate((sums_a[0:1, :], sums_b[0:1, :], sums_a[1:2, :], sums_b[1:2, :])):
+        side = jnp.where(rows == EXPERTS + i, value, side)
+    lane = lax.broadcasted_iota(jnp.int32, (model, LANES), 1)
+    small_ref[:, 4 * model :] = jnp.where(lane < EXPERTS, router_ref[...], jnp.transpose(side))
+
+
+def back_kernel(*refs):
+    ins, (grad_ref, small_ref), scratch = refs[:12], refs[12:14], refs[14:]
+    back(*ins, grad_ref, small_ref, scratch)
+
+
+def back_middle_kernel(*refs):
+    ins, (gates_ref, routed_ref, turned_ref) = refs[:12], refs[12:15]
+    grad_ref, small_ref, grad_gates_ref, leaving_ref = refs[15:19]
+    scratch, pairs_ref = refs[19:-1], refs[-1]
+    back(*ins, grad_ref, small_ref, scratch)
+    split_grads(grad_ref, gates_ref, routed_ref, turned_ref, pairs_ref, grad_gates_ref, leaving_ref)
+
+
+def shape(dims, kind):
+    return jax.ShapeDtypeStruct(dims, kind)
+
+
+def front_outs(model):
+    return [
+        shape((ROWS, model), F32),
+        shape((ROWS, 3 * model), BF16),
+        shape((ROWS, LANES), F32),
+        shape((ROWS, model), BF16),
+        shape((ROWS, LANES), jnp.int32),
+        shape((8, ROWS), jnp.int32),
+        shape((ROWS, LANES), F32),
+        shape((ROWS, LANES), F32),
+        shape((EXPERTS * CAP_PAD, model), BF16),
+    ]
+
+
+def back_scratch(model):
+    return [
+        pltpu.VMEM((ROWS, model), BF16),
+        pltpu.VMEM((ROWS, model), F32),
+        pltpu.VMEM((ROWS, 3 * model), BF16),
+        pltpu.VMEM((ROWS, model), BF16),
+        pltpu.VMEM((ROWS, model), BF16),
+        pltpu.VMEM((ROWS, model), F32),
+        pltpu.VMEM((2, model), F32),
+        pltpu.VMEM((2, model), F32),
+        pltpu.VMEM((model, LANES), F32),
+    ]
+
+
+def call(kernel, outs, scratch, name, limit=56):
+    return pl.pallas_call(
+        kernel,
+        out_shape=outs,
+        scratch_shapes=scratch,
+        compiler_params=pltpu.CompilerParams(vmem_limit_bytes=limit << 20),
+        name=name,
+    )
+
+
+def run_first(x, w, picks):
+    model = x.shape[1]
+    return call(first_kernel, front_outs(model), [pltpu.VMEM((ROWS, model), BF16)], "first")(x, w, picks)
+
+
+def run_middle(x1, gates, slots, returned, w, picks):
+    model = x1.shape[1]
+    outs = [shape((ROWS, model), F32), shape((TOP * ROWS, model), BF16)] + front_outs(model)
+    scratch = [pltpu.VMEM((ROWS, model), BF16), pltpu.VMEM((TOP * ROWS, model), F32)]
+    return call(middle_kernel, outs, scratch, "middle")(x1, gates, slots, returned, w, picks)
+
+
+def run_last(x1, gates, slots, turned, returned, teacher, scale):
+    model = x1.shape[1]
+    outs = [
+        shape((ROWS, model), BF16),
+        shape((ROWS, model), F32),
+        shape((ROWS, LANES), F32),
+        shape((EXPERTS * CAP_PAD, model), BF16),
+    ]
+    scratch = [
+        pltpu.VMEM((ROWS, model), F32),
+        pltpu.VMEM((TOP * ROWS, model), BF16),
+        pltpu.VMEM((TOP * ROWS, model), F32),
+        pltpu.VMEM((TOP * ROWS, model), BF16),
+    ]
+    return call(last_kernel, outs, scratch, "last")(x1, gates, slots, turned, returned, teacher, scale)
+
+
+def small_shape(model):
+    return shape((model, 4 * model + LANES), F32)
+
+
+def run_back(*ins):
+    model = ins[0].shape[1]
+    return call(back_kernel, [shape((ROWS, model), F32), small_shape(model)], back_scratch(model), "back")(*ins)
+
+
+def run_back_middle(*ins):
+    model = ins[0].shape[1]
+    outs = [shape((ROWS, model), F32), small_shape(model), shape((ROWS, LANES), F32), shape((EXPERTS * CAP_PAD, model), BF16)]
+    scratch = back_scratch(model) + [pltpu.VMEM((TOP * ROWS, model), BF16)]
+    return call(back_middle_kernel, outs, scratch, "back_middle")(*ins)
+
+
+TILE = 640
+WIDE = 512
+ROOT = 0.7978845608028654
+CUBE = 0.044715
+
+
+def expert_kernel(x_ref, in_ref, out_ref, made_ref, act_ref, slope_ref):
+    total = jnp.zeros((x_ref.shape[0], out_ref.shape[1]), F32)
+    for start in range(0, in_ref.shape[1], WIDE):
+        columns = slice(start, start + WIDE)
+        pre = dot(x_ref[...], in_ref[:, columns])
+        square = pre * pre
+        bend = jnp.tanh(pre * (ROOT + ROOT * CUBE * square))
+        half = 0.5 + 0.5 * bend
+        act = (pre * half).astype(BF16)
+        slope = half + (0.5 * pre) * (1.0 - bend * bend) * (ROOT + 3.0 * ROOT * CUBE * square)
+        act_ref[:, columns] = act
+        slope_ref[:, columns] = slope.astype(BF16)
+        total = total + dot(act, out_ref[columns, :])
+    made_ref[...] = total.astype(BF16)
+
+
+def run_expert(rows, weight_in, weight_out):
+    count, model = rows.shape
+    hidden = weight_in.shape[1]
+    whole = lambda dims: pl.BlockSpec(dims, lambda i: (0, 0), pipeline_mode=pl.Buffered(1))
+    tile = lambda width: pl.BlockSpec((TILE, width), lambda i: (i, 0))
+    return pl.pallas_call(
+        expert_kernel,
+        grid=(count // TILE,),
+        in_specs=[tile(model), whole((model, hidden)), whole((hidden, model))],
+        out_specs=[tile(model), tile(hidden), tile(hidden)],
+        out_shape=[shape((count, model), BF16), shape((count, hidden), BF16), shape((count, hidden), BF16)],
+        compiler_params=pltpu.CompilerParams(vmem_limit_bytes=56 << 20),
+        name="expert",
+    )(rows, weight_in, weight_out)
+
+
+def expert_back_kernel(x_ref, g_ref, act_ref, slope_ref, in_ref, out_ref, back_ref, gin_ref, gout_ref, total_ref, gpre_ref):
+    count = x_ref.shape[0]
+    step = pl.program_id(0)
+
+    @pl.when(step == 0)
+    def _():
+        total_ref[...] = jnp.zeros_like(total_ref)
+
+    def tile(i, carry):
+        rows = rows_of(i, TILE)
+        grad_act = dot_nt(g_ref[rows, :], out_ref[...])
+        grad_pre = (slope_ref[rows, :].astype(F32) * grad_act).astype(BF16)
+        gpre_ref[rows, :] = grad_pre
+        total_ref[rows, :] += dot_nt(grad_pre, in_ref[...])
+        return carry
+
+    lax.fori_loop(0, count // TILE, tile, 0)
+    gin_ref[...] = dot_tn(x_ref[...], gpre_ref[...]).astype(BF16)
+    gout_ref[...] = dot_tn(act_ref[...], g_ref[...]).astype(BF16)
+
+    @pl.when(step == pl.num_programs(0) - 1)
+    def _():
+        back_ref[...] = total_ref[...].astype(BF16)
+
+
+def run_expert_back(rows, grads, act, slope, weight_in, weight_out):
+    count, model = rows.shape
+    hidden = weight_in.shape[1]
+    whole = pl.BlockSpec((count, model), lambda i: (0, 0), pipeline_mode=pl.Buffered(1))
+    across = lambda height: pl.BlockSpec((height, WIDE), lambda i: (0, i))
+    down = pl.BlockSpec((WIDE, model), lambda i: (i, 0))
+    return pl.pallas_call(
+        expert_back_kernel,
+        grid=(hidden // WIDE,),
+        in_specs=[whole, whole, across(count), across(count), across(model), down],
+        out_specs=[pl.BlockSpec((count, model), lambda i: (0, 0)), across(model), down],
+        out_shape=[shape((count, model), BF16), shape((model, hidden), BF16), shape((hidden, model), BF16)],
+        scratch_shapes=[pltpu.VMEM((count, model), F32), pltpu.VMEM((count, WIDE), BF16)],
+        compiler_params=pltpu.CompilerParams(vmem_limit_bytes=56 << 20),
+        name="expert_back",
+    )(rows, grads, act, slope, weight_in, weight_out)
 
 
 def layer_norm(values, gain_row, shift_row):
@@ -343,6 +867,127 @@
     )
 
 
+def pad_rows(values, fill=0):
+    width = values.shape[-1]
+    images = values.reshape(SLOTS, SEQ, width)
+    images = jnp.pad(images, ((0, 0), (0, SEQ_PAD - SEQ), (0, 0)), constant_values=fill)
+    images = images.reshape(SLOTS * SEQ_PAD, width)
+    return jnp.pad(images, ((0, ROWS - SLOTS * SEQ_PAD), (0, 0)), constant_values=fill)
+
+
+def live_rows(values):
+    images = values[: SLOTS * SEQ_PAD].reshape(SLOTS, SEQ_PAD, values.shape[-1])
+    return images[:, :SEQ].reshape(SLOTS * SEQ, values.shape[-1])
+
+
+def exchange(rows):
+    blocks = rows.reshape(EXPERTS, CAP_PAD, rows.shape[-1])
+    moved = lax.all_to_all(blocks, ("expert", "shard"), split_axis=0, concat_axis=0, tiled=True)
+    return moved.reshape(rows.shape)
+
+
+def own_expert(shard_part):
+    moved = lax.all_to_all(shard_part, "shard", split_axis=0, concat_axis=0, tiled=True)
+    return moved.reshape(-1, shard_part.shape[-1])
+
+
+def share_expert(grad):
+    shards_all = lax.axis_size("shard")
+    blocks = grad.reshape(shards_all, grad.shape[0] // shards_all, grad.shape[1])
+    moved = lax.all_to_all(blocks, "shard", split_axis=0, concat_axis=0, tiled=True)
+    return moved.astype(F32)
+
+
+def owners(
+    states,
+    qkv_weight,
+    out_weight,
+    norm_gain,
+    norm_bias,
+    router_weight,
+    expert_in,
+    expert_out,
+    chosen,
+    image_count,
+    teacher,
+):
+    layers, share, _ = qkv_weight.shape
+    model = states.shape[1]
+    groups = lax.axis_size("expert")
+    piece = share // groups
+    spare = LANES - EXPERTS - 5
+    marks = jnp.zeros((layers, share, 1 + spare), BF16)
+    packed = jnp.concatenate(
+        [qkv_weight, out_weight, router_weight, norm_gain, norm_bias, marks], axis=2
+    )
+    packed = lax.dynamic_slice_in_dim(packed, lax.axis_index("expert") * piece, piece, 1)
+    mark_at = 4 * model + EXPERTS + 4
+    packed = packed.at[0, 0, mark_at].set(image_count[0].astype(BF16))
+    weights = [
+        lax.all_gather(packed[layer], ("shard", "expert"), axis=0, tiled=True)
+        for layer in range(layers)
+    ]
+    experts = [(own_expert(expert_in[layer]), own_expert(expert_out[layer])) for layer in range(layers)]
+    counted = jnp.sum(weights[0][:, mark_at].astype(F32)) * SEQ
+    slot_image = jnp.arange(states.shape[0], dtype=jnp.int32) // SEQ
+    living = slot_image < image_count[0]
+    scale = pad_rows(jnp.where(living, 2.0 / counted, 0.0)[:, None])
+    picks = [
+        jnp.pad(pad_rows(chosen[layer], -1), ((0, 0), (0, LANES - TOP)), constant_values=-1)
+        for layer in range(layers)
+    ]
+    kept = []
+    current = pad_rows(states.astype(F32))
+    fronts = run_first(current, weights[0], picks[0])
+    for layer in range(layers):
+        x1, proj, logs, att, slots, turned, chances, gates, leaving = fronts
+        arrived = exchange(leaving)
+        made, act, slope = run_expert(arrived, *experts[layer])
+        returned = exchange(made)
+        entry = [current, x1, proj, logs, att, slots, turned, chances, gates, arrived, act, slope, None]
+        kept.append(entry)
+        if layer + 1 < layers:
+            current, entry[12], *fronts = run_middle(
+                x1, gates, slots, returned, weights[layer + 1], picks[layer + 1]
+            )
+    final, grad, grad_gates, leaving = run_last(
+        x1, gates, slots, turned, returned, pad_rows(teacher), scale
+    )
+    smalls, ins, outs = [None] * layers, [None] * layers, [None] * layers
+    for layer in reversed(range(layers)):
+        current, x1, proj, logs, att, slots, turned, chances, gates, arrived, act, slope, _ = kept[layer]
+        came = exchange(leaving)
+        back_rows, grad_in, grad_out = run_expert_back(arrived, came, act, slope, *experts[layer])
+        returned = exchange(back_rows)
+        ins[layer], outs[layer] = share_expert(grad_in), share_expert(grad_out)
+        common = (grad, returned, slots, picks[layer], grad_gates, chances, x1, current, proj, logs, att, weights[layer])
+        if layer > 0:
+            below = kept[layer - 1]
+            grad, small, grad_gates, leaving = run_back_middle(*common, below[8], below[12], below[6])
+        else:
+            grad, small = run_back(*common)
+        part = lax.psum_scatter(small, ("shard", "expert"), scatter_dimension=0, tiled=True)
+        smalls[layer] = lax.all_gather(part, "expert", axis=0, tiled=True)
+    small = jnp.stack(smalls)
+    at = 4 * model
+    return (
+        live_rows(final),
+        live_rows(grad) * counted,
+        small[:, :, : 3 * model],
+        small[:, :, 3 * model : at],
+        small[:, :, at + EXPERTS : at + EXPERTS + 2],
+        small[:, :, at + EXPERTS + 2 : at + EXPERTS + 4],
+        small[:, :, at : at + EXPERTS],
+        jnp.stack(ins),
+        jnp.stack(outs),
+    )
+
+
+def plan_of(mesh):
+    groups, shards_all = mesh.shape["expert"], mesh.shape["shard"]
+    return owners if groups * shards_all == EXPERTS else shards
+
+
 def solution(mesh):
     in_specs = (
         P(("expert", "shard"), None),
@@ -368,4 +1013,4 @@
         P(None, "expert", "shard", None),
         P(None, "expert", "shard", None),
     )
-    return jax.shard_map(shards, mesh=mesh, in_specs=in_specs, out_specs=out_specs, check_vma=False)
+    return jax.shard_map(plan_of(mesh), mesh=mesh, in_specs=in_specs, out_specs=out_specs, check_vma=False)

time: 1970 us -> 1220 us (0.62)
  waiting for transfers between devices: 1110 us -> 446 us
  Pallas kernels: 0 us -> 255 us
  matrix products: 231 us -> 0 us
  local copies, waits for them, and re-layouts: 234 us -> 30.5 us
  blocking collectives: 248 us -> 398 us
  other arithmetic: 103 us -> 18.2 us
  starting transfers between devices: 21.2 us -> 47.9 us
    reduce_scatter x4 -> x2, waiting for transfers between devices: 579 us -> 12.1 us  [owners(): lax.psum_scatter(small, ('shard', 'expert'), scatter_dimension=0, tiled=T...]
    all_gather x6 -> x4, waiting for transfers between devices: 374 us -> 61.2 us  [the longest x2 36.2 us: owners(): smalls[layer] = lax.all_gather(part, 'expert', axis=0, tiled=True)]
    all_to_all x5 -> x10, waiting for transfers between devices: 77.6 us -> 371 us  [the longest x3 182 us: exchange(): lax.all_to_all(blocks, ('expert', 'shard'), split_axis=0, concat_axis=0,...]
    all_to_all x3 -> x6, blocking collectives: 107 us -> 398 us  [the longest x5 336 us: exchange(): lax.all_to_all(blocks, ('expert', 'shard'), split_axis=0, concat_axis=0,...]
    pallas_call x0 -> x9, Pallas kernels: none -> 255 us  [the longest x2 68.2 us: run_expert_back(): pl.pallas_call(expert_back_kernel, grid=(hidden // WIDE,), in_specs=[whol...]
    dot_general x42 -> x0, matrix products: 231 us -> none  [the longest x2 44.6 us: mixture_backward(): jnp.einsum('erd,ehd->erh', grad_result, out_full, preferred_element_type=...]
    psum x2 -> x0, blocking collectives: 98.2 us -> none  [the longest x1 60.8 us: shards(): lax.psum(image_count[0].astype(jnp.float32) * SEQ, ('expert', 'shard'))]
    psum x1 -> x0, waiting for transfers between devices: 74.4 us -> none  [shards(): lax.psum((mixer_grads[0], mixer_grads[1], mixer_grads[2], mixer_grads[3],...]
  transfers between devices with their start and end apart: 16 -> 16, of which waited for: 13 -> 15; matrix products, arithmetic and copies ran while one was open for 15% -> 3% of each run, Pallas kernels for 0% -> 12%
where the time goes in v1:
time: 1220 us; the launch traced here: 1210 us
  waiting for transfers between devices  446 us (37%)
  blocking collectives  398 us (33%)
  Pallas kernels  255 us (21%)
  starting transfers between devices  47.9 us (4%)
  local copies, waits for them, and re-layouts  30.5 us (2%)
  other arithmetic  18.2 us (1%)
  between operations  15.9 us (1%)
    all_to_all x5, blocking collectives, exchange(): lax.all_to_all(blocks, ('expert', 'shard'), split_axis=0, concat_axis=0,...  336 us
    all_to_all x3, waiting for transfers between devices, exchange(): lax.all_to_all(blocks, ('expert', 'shard'), split_axis=0, concat_axis=0,...  182 us
    all_to_all x3, waiting for transfers between devices, share_expert(): lax.all_to_all(blocks, 'shard', split_axis=0, concat_axis=0, tiled=True)  98.3 us
    all_to_all x4, waiting for transfers between devices, own_expert(): lax.all_to_all(shard_part, 'shard', split_axis=0, concat_axis=0, tiled=True)  90.7 us
    pallas_call x2, Pallas kernels, run_expert_back(): pl.pallas_call(expert_back_kernel, grid=(hidden // WIDE,), in_specs=[whol...  68.2 us
    all_to_all x1, blocking collectives, share_expert(): lax.all_to_all(blocks, 'shard', split_axis=0, concat_axis=0, tiled=True)  61.9 us
    pallas_call x2, Pallas kernels, run_expert(): pl.pallas_call(expert_kernel, grid=(count // TILE,), in_specs=[tile(model...  46.9 us
    pallas_call x1, Pallas kernels, run_back_middle(): return call(back_middle_kernel, outs, scratch, 'back_middle')(*ins)  41.4 us
  transfers between devices with their start and end apart: 16, of which 15 were waited for; matrix products, arithmetic and copies ran while one was open for 3% of the time, Pallas kernels for 12%

profile of v1, /device:TPU:0, one launch (start us, length us, event | category | flops | bytes accessed | tf_op | source)
XLA Modules:
  0.0 1212.0 jit_solution(2760157184938343174)
XLA Ops:
  7.2 4.8 slice_bitcast_fusion.1
  12.0 6.5 all-to-all-start.1
  19.2 0.8 copy.29
  19.9 0.8 copy.30
  21.5 2.3 concatenate.6
  24.6 4.5 slice_bitcast_fusion
  29.1 39.9 %all-to-all-done.1 = bf16[4,128,2048]{2,1,0:T(8,128)(2,1)S(1)} async-done(((bf16[4,128,2048]{2,1,0:T(8,128)(2,1)}), bf16[4,128,2048]{2,1,0:T(8,128)(2,1)S(1)}, u32[]{:S(2)}, u32[]{:S(2)}) %all-to-all-start.1) | async-done | bytes 2097184 | tf_op jit(solution)/shard_map/all_to_all | solution.py:890
  69.1 1.4 copy-done
  70.5 4.5 all-to-all-start.2
  75.3 0.7 pad.71.picks_ref.refs_3_
  76.2 1.2 pad_convert_fusion.x_ref.refs_7_
  77.5 22.4 %all-gather.11.cloned.1.call-done = bf16[1,512,2176]{2,1,0:T(8,128)(2,1)} async-done(((bf16[1,16,2176]{2,1,0:T(8,128)(2,1)}), bf16[1,512,2176]{2,1,0:T(8,128)(2,1)}) %all-gather.11.cloned.1.call-update) | async-done | bytes 2228240 | tf_op jit(solution)/shard_map/all_gather | solution.py:927
  99.8 20.2 %first.1 = (f32[640,512]{1,0:T(8,128)}, bf16[640,1536]{1,0:T(8,128)(2,1)}, f32[640,128]{1,0:T(8,128)}, bf16[640,512]{1,0:T(8,128)(2,1)}, s32[640,128]{1,0:T(8,12...) custom-call(f32[640,512]{1,0:T(8,128)} %pad_convert_fusion.x_ref.refs_7_, ...), custom_call_target="tpu_custom_call" | custom-call | tf_op jit(solution)/shard_map/first/pallas_call | solution.py:418
  120.0 7.9 all-to-all-done.2
  127.9 74.1 %all_to_all.80 = bf16[32,80,512]{2,1,0:T(8,128)(2,1)} all-to-all(bf16[32,80,512]{2,1,0:T(8,128)(2,1)} %bitcast.91), channel_id=1, replica_groups=mesh['expert'=8,'shard'=4] {'expert','shard'}, dimensions={0} | all-to-all | bytes 5242880 | tf_op jit(solution)/shard_map/all_to_all | solution.py:885
  201.9 4.2 all-to-all-start.5
  206.1 23.4 %expert.2 = (bf16[2560,512]{1,0:T(8,128)(2,1)}, bf16[2560,2048]{1,0:T(8,128)(2,1)}, bf16[2560,2048]{1,0:T(8,128)(2,1)}) custom-call(bf16[2560,512]{1,0:T(8,128)(2,1)} %bitcast.56, bf16[512,2048]{1,0:T(8,128)(2,1)} %bitcast.60, bf16[2048,512]{1,0:T(8,128)(2,1)} %bitcast.10.out_ref), custom_call_target="tpu_custom_call" | custom-call | tf_op jit(solution)/shard_map/expert/pallas_call | solution.py:488
  229.6 25.9 %all-to-all-done.5 = bf16[4,128,2048]{2,1,0:T(8,128)(2,1)S(1)} async-done(((bf16[4,128,2048]{2,1,0:T(8,128)(2,1)}), bf16[4,128,2048]{2,1,0:T(8,128)(2,1)S(1)}, u32[]{:S(2)}, u32[]{:S(2)}) %all-to-all-start.5) | async-done | bytes 2097184 | tf_op jit(solution)/shard_map/all_to_all | solution.py:890
  255.4 1.4 copy-done.1
  256.8 3.5 all-to-all-start.3
  260.4 0.7 all-gather.13.cloned.1.call-update
  261.1 64.4 %all-to-all-done.3 = bf16[32,80,512]{2,1,0:T(8,128)(2,1)} async-done(((bf16[32,80,512]{2,1,0:T(8,128)(2,1)}), bf16[32,80,512]{2,1,0:T(8,128)(2,1)}, u32[]{:S(2)}, u32[]{:S(2)}) %all-to-all-start.3) | async-done | bytes 2621472 | tf_op jit(solution)/shard_map/all_to_all | solution.py:885
  325.5 6.0 all-to-all-start.6
  331.8 0.8 pad.72.picks_ref.refs_3_
  332.6 2.6 all-gather.13.cloned.1.call-done
  335.1 27.5 %middle.1 = (f32[640,512]{1,0:T(8,128)}, bf16[1280,512]{1,0:T(8,128)(2,1)}, f32[640,512]{1,0:T(8,128)}, bf16[640,1536]{1,0:T(8,128)(2,1)}, f32[640,128]{1,0:T(8,...) custom-call(f32[640,512]{1,0:T(8,128)} %get-tuple-element.63.x1_ref., ...), custom_call_target="tpu_custom_call" | custom-call | tf_op jit(solution)/shard_map/middle/pallas_call | solution.py:425
  362.6 17.0 %all-to-all-done.6 = bf16[4,512,512]{2,1,0:T(8,128)(2,1)S(1)} async-done(((bf16[4,512,512]{2,1,0:T(8,128)(2,1)}), bf16[4,512,512]{2,1,0:T(8,128)(2,1)S(1)}, u32[]{:S(2)}, u32[]{:S(2)}) %all-to-all-start.6) | async-done | bytes 2097184 | tf_op jit(solution)/shard_map/all_to_all | solution.py:890
  379.7 62.9 %all_to_all.81 = bf16[32,80,512]{2,1,0:T(8,128)(2,1)} all-to-all(bf16[32,80,512]{2,1,0:T(8,128)(2,1)} %bitcast.90), channel_id=1, replica_groups=mesh['expert'=8,'shard'=4] {'expert','shard'}, dimensions={0} | all-to-all | bytes 5242880 | tf_op jit(solution)/shard_map/all_to_all | solution.py:885
  442.6 23.4 %expert.3 = (bf16[2560,512]{1,0:T(8,128)(2,1)}, bf16[2560,2048]{1,0:T(8,128)(2,1)}, bf16[2560,2048]{1,0:T(8,128)(2,1)}) custom-call(bf16[2560,512]{1,0:T(8,128)(2,1)} %bitcast.58, bf16[512,2048]{1,0:T(8,128)(2,1)} %bitcast.62, bf16[2048,512]{1,0:T(8,128)(2,1)} %bitcast.64), custom_call_target="tpu_custom_call" | custom-call | tf_op jit(solution)/shard_map/expert/pallas_call | solution.py:488
  466.0 4.2 all-to-all-start.7
  470.2 1.2 reshape.223
  471.5 0.9 pad.62.teacher_ref
  472.4 1.6 convert_reduce_fusion
  475.0 0.7 pad.64.scale_ref
  475.7 53.1 %all-to-all-done.7 = bf16[32,80,512]{2,1,0:T(8,128)(2,1)S(1)} async-done(((bf16[32,80,512]{2,1,0:T(8,128)(2,1)}), bf16[32,80,512]{2,1,0:T(8,128)(2,1)S(1)}, u32[]{:S(2)}, u32[]{:S(2)}) %all-to-all-start.7) | async-done | bytes 2621472 | tf_op jit(solution)/shard_map/all_to_all | solution.py:885
  528.8 1.5 copy-done.5
  530.3 16.8 %last.1 = (bf16[640,512]{1,0:T(8,128)(2,1)}, f32[640,512]{1,0:T(8,128)}, f32[640,128]{1,0:T(8,128)}, bf16[2560,512]{1,0:T(8,128)(2,1)}) custom-call(f32[640,512]{1,0:T(8,128)} %get-tuple-element.68.x1_ref.refs_6_, f32[640,128]{1,0:T(8,128)} %get-tuple-element.69.gates_ref, s32[640,128]{1,0:T(8,128)} %get-tuple-element.70.slots_ref.refs_2_, ...), custom_call_target="tpu_custom_call" | custom-call | tf_op jit(solution)/shard_map/last/pallas_call | solution.py:442
  547.1 63.8 %all_to_all.82 = bf16[32,80,512]{2,1,0:T(8,128)(2,1)} all-to-all(bf16[32,80,512]{2,1,0:T(8,128)(2,1)} %bitcast.92), channel_id=1, replica_groups=mesh['expert'=8,'shard'=4] {'expert','shard'}, dimensions={0} | all-to-all | bytes 5242880 | tf_op jit(solution)/shard_map/all_to_all | solution.py:885
  610.9 34.1 %expert_back.2 = (bf16[2560,512]{1,0:T(8,128)(2,1)}, bf16[512,2048]{1,0:T(8,128)(2,1)}, bf16[2048,512]{1,0:T(8,128)(2,1)}) custom-call(bf16[2560,512]{1,0:T(8,128)(2,1)} %bitcast.59, bf16[2560,512]{1,0:T(8,128)(2,1)} %bitcast.78, bf16[2560,2048]{1,0:T(8,128)(2,1)} %get-tuple-element.77.act_ref, bf16[2560,2048]{1,0:T(8,128)(2,1)} %get-tuple-element.78.slope_ref, ...), custom_call_target="tpu_custom_call" | custom-call | tf_op jit(solution)/shard_map/expert_back/pallas_call | solution.py:530
  645.0 63.5 %all_to_all.83 = bf16[32,80,512]{2,1,0:T(8,128)(2,1)} all-to-all(bf16[32,80,512]{2,1,0:T(8,128)(2,1)} %bitcast.93), channel_id=1, replica_groups=mesh['expert'=8,'shard'=4] {'expert','shard'}, dimensions={0} | all-to-all | bytes 5242880 | tf_op jit(solution)/shard_map/all_to_all | solution.py:885
  708.5 41.4 %back_middle.1 = (f32[640,512]{1,0:T(8,128)}, f32[512,2176]{1,0:T(8,128)}, f32[640,128]{1,0:T(8,128)}, bf16[2560,512]{1,0:T(8,128)(2,1)}) custom-call(f32[640,512]{1,0:T(8,128)} %get-tuple-element.75.refs_0_, bf16[2560,512]{1,0:T(8,128)(2,1)} %bitcast.74, s32[640,128]{1,0:T(8,128)} %get-tuple-element.70.slots_ref.refs_2_, s32[640,128]{1,0:T(8,128)} %pad.72.picks_ref.refs_3_, ...), custom_call_target="tpu_custom_call" | custom-call | tf_op jit(solution)/shard_map/back_middle/pallas_call | solution.py:458
  749.9 4.2 all-to-all-start.10
  754.8 64.3 %all-to-all-done.10 = bf16[32,80,512]{2,1,0:T(8,128)(2,1)S(1)} async-done(((bf16[32,80,512]{2,1,0:T(8,128)(2,1)}), bf16[32,80,512]{2,1,0:T(8,128)(2,1)S(1)}, u32[]{:S(2)}, u32[]{:S(2)}) %all-to-all-start.10) | async-done | bytes 2621472 | tf_op jit(solution)/shard_map/all_to_all | solution.py:885
  819.1 1.5 copy-done.6
  820.6 34.1 %expert_back.3 = (bf16[2560,512]{1,0:T(8,128)(2,1)}, bf16[512,2048]{1,0:T(8,128)(2,1)}, bf16[2048,512]{1,0:T(8,128)(2,1)}) custom-call(bf16[2560,512]{1,0:T(8,128)(2,1)} %bitcast.57, bf16[2560,512]{1,0:T(8,128)(2,1)} %bitcast.77, bf16[2560,2048]{1,0:T(8,128)(2,1)} %get-tuple-element.90.act_ref, bf16[2560,2048]{1,0:T(8,128)(2,1)} %get-tuple-element.91.slope_ref, ...), custom_call_target="tpu_custom_call" | custom-call | tf_op jit(solution)/shard_map/expert_back/pallas_call | solution.py:530
  854.7 72.0 %all_to_all.84 = bf16[32,80,512]{2,1,0:T(8,128)(2,1)} all-to-all(bf16[32,80,512]{2,1,0:T(8,128)(2,1)} %bitcast.94), channel_id=1, replica_groups=mesh['expert'=8,'shard'=4] {'expert','shard'}, dimensions={0} | all-to-all | bytes 5242880 | tf_op jit(solution)/shard_map/all_to_all | solution.py:885
  926.7 4.3 all-to-all-start.13
  931.0 34.5 %back.1 = (f32[640,512]{1,0:T(8,128)}, f32[512,2176]{1,0:T(8,128)}) custom-call(f32[640,512]{1,0:T(8,128)} %get-tuple-element.88.refs_0_, bf16[2560,512]{1,0:T(8,128)(2,1)} %bitcast.76, s32[640,128]{1,0:T(8,128)} %get-tuple-element.65.slots_ref.refs_2_, s32[640,128]{1,0:T(8,128)} %pad.71.picks_ref.refs_3_, f32[640,128]{1,0:T(8,128)} %get-tuple-element.93.refs_4_, ...), custom_call_target="tpu_custom_call" | custom-call | tf_op jit(solution)/shard_map/back/pallas_call | solution.py:451
  965.6 16.0 %all-to-all-done.13 = bf16[4,128,2048]{2,1,0:T(8,128)(2,1)S(1)} async-done(((bf16[4,128,2048]{2,1,0:T(8,128)(2,1)}), bf16[4,128,2048]{2,1,0:T(8,128)(2,1)S(1)}, u32[]{:S(2)}, u32[]{:S(2)}) %all-to-all-start.13) | async-done | bytes 2097184 | tf_op jit(solution)/shard_map/all_to_all | solution.py:897
  981.6 61.9 %all_to_all.85 = bf16[4,512,512]{2,1,0:T(8,128)(2,1)} all-to-all(bf16[4,512,512]{2,1,0:T(8,128)(2,1)} %bitcast.99), channel_id=1, replica_groups=mesh['expert'=8,'shard'=4] {'shard'}, dimensions={0} | all-to-all | bytes 4194304 | tf_op jit(solution)/shard_map/all_to_all | solution.py:897
  1043.5 4.5 all-to-all-start.14
  1048.5 52.5 %all-to-all-done.14 = bf16[4,512,512]{2,1,0:T(8,128)(2,1)} async-done(((bf16[4,512,512]{2,1,0:T(8,128)(2,1)}), bf16[4,512,512]{2,1,0:T(8,128)(2,1)}, u32[]{:S(2)}, u32[]{:S(2)}) %all-to-all-start.14) | async-done | bytes 2097184 | tf_op jit(solution)/shard_map/all_to_all | solution.py:897
  1101.1 5.8 all-to-all-start.12
  1106.9 12.1 reduce-scatter.3.cloned.1.call-done
  1119.1 1.0 reshape.227
  1120.1 6.2 maximum_convert_fusion.1
  1126.3 29.8 %all-to-all-done.12 = bf16[4,128,2048]{2,1,0:T(8,128)(2,1)} async-done(((bf16[4,128,2048]{2,1,0:T(8,128)(2,1)}), bf16[4,128,2048]{2,1,0:T(8,128)(2,1)}, u32[]{:S(2)}, u32[]{:S(2)}) %all-to-all-start.12) | async-done | bytes 2097184 | tf_op jit(solution)/shard_map/all_to_all | solution.py:897
  1156.0 5.7 maximum_convert_fusion
  1162.0 1.2 mul.19
  1163.1 10.8 all-gather.9.cloned.1.call-done
  1173.9 25.4 %all-gather.7.cloned.1.call-done = f32[128,2176]{1,0:T(8,128)} async-done(((f32[16,2176]{1,0:T(8,128)}), f32[128,2176]{1,0:T(8,128)}) %all-gather.7.cloned.1.call-update) | async-done | bytes 1114128 | tf_op jit(solution)/shard_map/all_gather | solution.py:970
  1199.3 1.0 pad_maximum_fusion
  1200.8 0.9 fusion.1
  1201.6 1.3 fusion
  (64 shorter events, 6.8 us)
Async XLA Ops:
  12.0 7.2 copy-start.13
  12.0 7.9 copy-start.14
  12.0 8.7 copy-start.11
  12.0 9.5 copy-start.10
  12.0 57.1 %all-to-all-start.1 = ((bf16[4,128,2048]{2,1,0:T(8,128)(2,1)}), bf16[4,128,2048]{2,1,0:T(8,128)(2,1)S(1)}, u32[]{:S(2)}, u32[]{:S(2)}) async-start(bf16[4,128,2048]{2,1,0:T(8,128)(2,1)} %get-tuple-element.126), calls=%async_computation.1 | async-start | bytes 4194304 | tf_op jit(solution)/shard_map/all_to_all | solution.py:890
  18.5 81.3 %all-gather.11.cloned.1.call-start = ((), (), s32[]{:S(2)}) async-start(), calls=%async_computation.22 | async-start | bytes 2297856 | tf_op jit(solution)/shard_map/all_gather | solution.py:927
  69.1 1.4 copy-start
  69.1 5.9 copy-start.12
  69.1 6.9 copy-start.9
  70.5 57.4 %all-to-all-start.2 = ((bf16[4,512,512]{2,1,0:T(8,128)(2,1)}), bf16[4,512,512]{2,1,0:T(8,128)(2,1)}, u32[]{:S(2)}, u32[]{:S(2)}) async-start(bf16[4,512,512]{2,1,0:T(8,128)(2,1)} %get-tuple-element.124), calls=%async_computation.2 | async-start | bytes 4194304 | tf_op jit(solution)/shard_map/all_to_all | solution.py:890
  201.9 53.5 %all-to-all-start.5 = ((bf16[4,128,2048]{2,1,0:T(8,128)(2,1)}), bf16[4,128,2048]{2,1,0:T(8,128)(2,1)S(1)}, u32[]{:S(2)}, u32[]{:S(2)}) async-start(bf16[4,128,2048]{2,1,0:T(8,128)(2,1)} %get-tuple-element.125), calls=%async_computation.5 | async-start | bytes 4194304 | tf_op jit(solution)/shard_map/all_to_all | solution.py:890
  255.4 1.4 copy-start.1
  256.8 68.7 %all-to-all-start.3 = ((bf16[32,80,512]{2,1,0:T(8,128)(2,1)}), bf16[32,80,512]{2,1,0:T(8,128)(2,1)}, u32[]{:S(2)}, u32[]{:S(2)}) async-start(bf16[32,80,512]{2,1,0:T(8,128)(2,1)} %bitcast.89), calls=%async_computation.3 | async-start | bytes 5242880 | tf_op jit(solution)/shard_map/all_to_all | solution.py:885
  260.4 74.8 %all-gather.13.cloned.1.call-start = ((), (), s32[]{:S(2)}) async-start(), calls=%async_computation.23 | async-start | bytes 2297856 | tf_op jit(solution)/shard_map/all_gather | solution.py:927
  325.5 54.1 %all-to-all-start.6 = ((bf16[4,512,512]{2,1,0:T(8,128)(2,1)}), bf16[4,512,512]{2,1,0:T(8,128)(2,1)S(1)}, u32[]{:S(2)}, u32[]{:S(2)}) async-start(bf16[4,512,512]{2,1,0:T(8,128)(2,1)} %get-tuple-element.123), calls=%async_computation.6 | async-start | bytes 4194304 | tf_op jit(solution)/shard_map/all_to_all | solution.py:890
  379.7 63.0 %copy-start.2 = (bf16[4,512,512]{2,1,0:T(8,128)(2,1)}, bf16[4,512,512]{2,1,0:T(8,128)(2,1)S(1)}, u32[]{:S(2)}) copy-start(bf16[4,512,512]{2,1,0:T(8,128)(2,1)S(1)} %all-to-all-done.6) | copy-start | bytes 6291460
  466.0 62.8 %all-to-all-start.7 = ((bf16[32,80,512]{2,1,0:T(8,128)(2,1)}), bf16[32,80,512]{2,1,0:T(8,128)(2,1)S(1)}, u32[]{:S(2)}, u32[]{:S(2)}) async-start(bf16[32,80,512]{2,1,0:T(8,128)(2,1)} %bitcast.88), calls=%async_computation.7 | async-start | bytes 5242880 | tf_op jit(solution)/shard_map/all_to_all | solution.py:885
  528.8 1.5 copy-start.5
  749.9 69.2 %all-to-all-start.10 = ((bf16[32,80,512]{2,1,0:T(8,128)(2,1)}), bf16[32,80,512]{2,1,0:T(8,128)(2,1)S(1)}, u32[]{:S(2)}, u32[]{:S(2)}) async-start(bf16[32,80,512]{2,1,0:T(8,128)(2,1)} %bitcast.87), calls=%async_computation.10 | async-start | bytes 5242880 | tf_op jit(solution)/shard_map/all_to_all | solution.py:885
  754.1 293.9 %reduce-scatter.5.cloned.1.call-start = ((), (), s32[]{:S(2)}) async-start(), calls=%async_computation.20 | async-start | bytes 4595712 | tf_op jit(solution)/shard_map/reduce_scatter | solution.py:969
  819.1 1.5 copy-start.6
  926.7 54.9 %all-to-all-start.13 = ((bf16[4,128,2048]{2,1,0:T(8,128)(2,1)}), bf16[4,128,2048]{2,1,0:T(8,128)(2,1)S(1)}, u32[]{:S(2)}, u32[]{:S(2)}) async-start(bf16[4,128,2048]{2,1,0:T(8,128)(2,1)} %bitcast.100), calls=%async_computation.15 | async-start | bytes 4194304 | tf_op jit(solution)/shard_map/all_to_all | solution.py:897
  931.0 188.0 %reduce-scatter.3.cloned.1.call-start = ((), (), s32[]{:S(2)}) async-start(), calls=%async_computation.18 | async-start | bytes 4595712 | tf_op jit(solution)/shard_map/reduce_scatter | solution.py:969
  1043.5 57.6 %all-to-all-start.14 = ((bf16[4,512,512]{2,1,0:T(8,128)(2,1)}), bf16[4,512,512]{2,1,0:T(8,128)(2,1)}, u32[]{:S(2)}, u32[]{:S(2)}) async-start(bf16[4,512,512]{2,1,0:T(8,128)(2,1)} %bitcast.101), calls=%async_computation.16 | async-start | bytes 4194304 | tf_op jit(solution)/shard_map/all_to_all | solution.py:897
  1047.9 126.0 %all-gather.9.cloned.1.call-start = ((), (), s32[]{:S(2)}) async-start(), calls=%async_computation.21 | async-start | bytes 1253376 | tf_op jit(solution)/shard_map/all_gather | solution.py:970
  1101.1 18.0 %copy-start.8 = (bf16[640,512]{1,0:T(8,128)(2,1)S(1)}, bf16[640,512]{1,0:T(8,128)(2,1)}, u32[]{:S(2)}) copy-start(bf16[640,512]{1,0:T(8,128)(2,1)} %get-tuple-element.74) | copy-start | bytes 1966084
  1101.1 55.0 %all-to-all-start.12 = ((bf16[4,128,2048]{2,1,0:T(8,128)(2,1)}), bf16[4,128,2048]{2,1,0:T(8,128)(2,1)}, u32[]{:S(2)}, u32[]{:S(2)}) async-start(bf16[4,128,2048]{2,1,0:T(8,128)(2,1)} %bitcast.98), calls=%async_computation.14 | async-start | bytes 4194304 | tf_op jit(solution)/shard_map/all_to_all | solution.py:897
  1106.9 92.4 %all-gather.7.cloned.1.call-start = ((), (), s32[]{:S(2)}) async-start(), calls=%async_computation.19 | async-start | bytes 1253376 | tf_op jit(solution)/shard_map/all_gather | solution.py:970
  1156.0 5.7 copy-start.7
  1173.9 26.4 %copy-start.3 = (f32[128,2176]{1,0:T(8,128)S(1)}, f32[128,2176]{1,0:T(8,128)}, u32[]{:S(2)}) copy-start(f32[128,2176]{1,0:T(8,128)} %all-gather.9.cloned.1.call-done) | copy-start | bytes 3342340
  1199.3 1.3 copy-start.4
Sparse Core Ops, SparseCore 0:
  24.7 75.0 all-gather.10
  264.0 71.0 all-gather.12
  757.8 153.4 reduce-scatter.4
  965.7 153.2 reduce-scatter.2
  1120.7 53.1 all-gather.8
  1175.6 23.6 all-gather.6
